TPU v7x, 512 devices: a whole 4x8x8 slice. The times are simulated.
512 devices in a mesh: dp: 128 (over z, y, core), expert: 4 (over x).
Axes of the slice: x: 4, y: 8, z: 8, core: 2. Of those that a mesh axis runs over, the one named last changes fastest.
Arguments:
- expert_grads: bfloat16 [128, 4, 1024, 896], P('dp', 'expert'), may hold values from -768 to 768
- round_offsets: int32 [128, 4, 1024], P('dp', 'expert'), may hold values from 0 to 1073741823
- slot_expert: int32 [4], replicated, may hold values from 0 to 3, each once
- master_weight: float32 [4, 1024, 896], P('expert', 'dp'), may hold values from -0.1875 to 0.1875
Outputs:
- mean_grad: float32 [4, 1024, 896], P('expert', 'dp')
- new_weight: float32 [4, 1024, 896], P('expert', 'dp')
- block_step: float32 [4, 128], P('expert', 'dp')
Inputs may be any that keep to these rules, and one draw needn't show every extreme that they name: `slot_expert`: each of 0 to 3 appears once.
All inputs are finite; a program needn't handle non-finite values.
Results may differ from a plain program's by a relative error of at most 0.0003.
Values may be sent and summed in bfloat16 or wider, within the bound.
A program may use at most 64 MiB of HBM per device.

v0:
```python
import jax
import jax.numpy as jnp
from jax import lax
from jax.sharding import Mesh
from jax.sharding import PartitionSpec as P

DP = ("dp_0", "dp_1", "dp_2")


level_bits = 6
low_power = -30
high_power = 30
learn_rate = 0.05


def split_up(array, dim, devices):
    before, after = (array.shape[:dim], array.shape[dim + 1 :])
    return jnp.moveaxis(array.reshape(*before, devices, -1, *after), dim, 0)


def laid_out(pieces, dim):
    shape = list(pieces.shape[1:])
    shape[dim] *= pieces.shape[0]
    return jnp.moveaxis(pieces, 0, dim).reshape(shape)


def moved_by_axis(pieces, axes, sequence):
    shape = [lax.axis_size(a) for a in axes]
    pieces = pieces.reshape(*shape, *pieces.shape[1:])
    for k in sequence:
        pieces = lax.all_to_all(pieces, axes[k], split_axis=k, concat_axis=k, tiled=True)
    return pieces.reshape(-1, *pieces.shape[len(axes) :])


def core_and_chips(array, groups, sequence, split_dim, concat_dim):
    devices = lax.axis_size(groups[0]) * lax.axis_size(groups[1])
    pieces = split_up(array, split_dim, devices)
    return laid_out(moved_by_axis(pieces, groups, sequence), concat_dim)


def in_one_piece(arrays, axis, dim, along):
    columns = [a.reshape(*a.shape[:along], -1) for a in arrays]
    both = jnp.concatenate(columns, axis=along)
    out, at, outs = (lax.all_gather(both, axis, axis=dim, tiled=True), 0, [])
    for a, column in zip(arrays, columns):
        slab = out[..., at : at + column.shape[along]]
        outs.append(slab.reshape(*slab.shape[:along], *a.shape[along:]))
        at += column.shape[along]
    return tuple(outs)


def power_steps(maxima):
    powers = jnp.array([2.0**exponent for exponent in range(low_power, high_power)], jnp.float32)
    reached = maxima[..., None] >= powers
    doubled = jnp.prod(jnp.where(reached, jnp.float32(2.0), jnp.float32(1.0)), axis=-1)
    return 2.0 ** (low_power - level_bits) * doubled


def dither(element_code):
    mixed = element_code * 747796405 + 1013904223
    mixed = jnp.bitwise_xor(mixed, jnp.right_shift(mixed, 13))
    mixed = mixed * 1103515245
    mixed = jnp.bitwise_xor(mixed, jnp.right_shift(mixed, 16))
    return jnp.bitwise_and(jnp.right_shift(mixed, 12), 255).astype(jnp.float32) / 256.0


def quantize(values, inverse_step, offsets):
    columns = lax.broadcasted_iota(jnp.int32, (1, values.shape[-1]), 1)
    element_code = offsets.astype(jnp.int32)[..., None] + columns
    scaled = values * inverse_step
    floor_part = jnp.floor(scaled)
    return (floor_part + jnp.floor(scaled - floor_part + dither(element_code))).astype(jnp.int32)


def body(expert_grads, round_offsets, slot_expert, master_weight):
    dp_count = lax.axis_size(DP)
    local_grads = expert_grads[0]
    slot_count = local_grads.shape[0]
    arrived, arrived_offsets = (
        core_and_chips(expert_grads, (("dp_0", "dp_1"), "dp_2"), (1, 0), 2, 0),
        core_and_chips(round_offsets, (("dp_0", "dp_1"), "dp_2"), (1, 0), 2, 0),
    )
    maxima = jnp.max(jnp.abs(arrived), axis=(0, 2, 3)).astype(jnp.float32)
    step_sizes = power_steps(maxima)[:, None]
    inverse_step = (1.0 / step_sizes)[None, :, :, None]
    counts = quantize(arrived.astype(jnp.float32), inverse_step, arrived_offsets)
    totals = jnp.sum(counts, axis=0, dtype=jnp.int32)
    mean_slot = totals.astype(jnp.float32) * (step_sizes / dp_count)[..., None]
    gathered, gathered_steps = in_one_piece((mean_slot, step_sizes), "expert", 0, 1)
    wanted = lax.axis_index("expert") * slot_count + lax.broadcasted_iota(
        jnp.int32, (slot_count, 1), 0
    )
    positions = lax.broadcasted_iota(jnp.int32, (1, slot_expert.shape[0]), 1)
    holder = jnp.sum(jnp.where(slot_expert[None, :] == wanted, positions, 0), axis=1)
    mean_grad = gathered[holder]
    block_step = gathered_steps[holder]
    new_weight = master_weight - learn_rate * mean_grad
    return (mean_grad, new_weight, block_step)


def solution(mesh):
    finer = Mesh(
        mesh.devices.reshape(8, 8, 2, mesh.shape["expert"]), ("dp_0", "dp_1", "dp_2", "expert")
    )
    return jax.shard_map(
        body,
        mesh=finer,
        in_specs=(P(DP, "expert", None, None), P(DP, "expert", None), P(), P("expert", DP, None)),
        out_specs=(P("expert", DP, None), P("expert", DP, None), P("expert", DP)),
        check_vma=False,
    )
```

profile of v0, /device:TPU:6, one launch (start us, length us, event | category | flops | bytes accessed | tf_op | source)
XLA Modules:
  0.0 116.0 jit_solution(14961913079614175007)
XLA Ops:
  0.6 2.9 %copy.11 = bf16[64,2,1,1,8,896]{5,4,0,3,2,1:T(8,128)(2,1)} copy(bf16[64,2,1,1,8,896]{5,4,1,0,3,2:T(8,128)(2,1)} %bitcast.22) | data formatting | bytes 3670016 | tf_op jit(solution)/shard_map/reshape;transpose;reshape | solution.py:29
  3.5 0.0 copy-start.1
  3.5 3.8 %all-to-all-start = ((bf16[64,2,1,1,8,896]{5,4,0,3,2,1:T(8,128)(2,1)}), bf16[64,2,1,1,8,896]{5,4,0,3,2,1:T(8,128)(2,1)S(1)}, u32[]{:S(2)}, u32[]{:S(2)}) async-start(bf16[64,2,1,1,8,896]{5,4,0,3,2,1:T(8,128)(2,1)} %copy.11), calls=%async_computation | async-start | bytes 3670016 | tf_op jit(solution)/shard_map/all_to_all | solution.py:31
  7.4 0.5 broadcast.150
  7.9 0.0 copy-done.1
  7.9 0.7 reduce.11
  8.6 0.1 reshape_transpose_reshape.7
  8.7 0.1 copy.13
  8.8 0.7 reshape.190
  9.5 0.6 all-to-all-done
  10.1 3.2 %all-to-all-start.2 = ((s32[2,1,512]{2,1,0:T(1,128)}), s32[2,1,512]{2,1,0:T(1,128)S(1)}, u32[]{:S(2)}, u32[]{:S(2)}) async-start(s32[2,1,512]{2,1,0:T(1,128)} %reshape.190), calls=%async_computation.2 | async-start | bytes 8192 | tf_op jit(solution)/shard_map/all_to_all | solution.py:31
  13.3 1.4 %copy.12 = bf16[64,2,1,1,8,896]{5,4,1,3,2,0:T(8,128)(2,1)} copy(bf16[64,2,1,1,8,896]{5,4,0,3,2,1:T(8,128)(2,1)S(1)} %all-to-all-done) | data formatting | bytes 3670016 | tf_op jit(solution)/shard_map/all_to_all | solution.py:31
  14.7 0.0 all-to-all-done.2
  14.7 16.7 %all-to-all-start.1 = ((bf16[64,2,1,1,8,896]{5,4,1,3,2,0:T(8,128)(2,1)}), bf16[64,2,1,1,8,896]{5,4,1,3,2,0:T(8,128)(2,1)S(1)}, u32[]{:S(2)}, u32[]{:S(2)}) async-start(bf16[64,2,1,1,8,896]{5,4,1,3,2,0:T(8,128)(2,1)} %copy.12), calls=%async_computation.1 | async-start | bytes 3670016 | tf_op jit(solution)/shard_map/all_to_all | solution.py:31
  31.4 0.0 copy-start.3
  31.4 0.5 broadcast.151
  31.9 0.7 reduce.12
  32.6 0.1 reshape.191
  32.7 0.7 copy.14
  33.4 0.0 copy-done.2
  33.4 0.6 fusion.10
  36.0 43.0 %all-to-all-done.1 = bf16[64,2,1,1,8,896]{5,4,1,3,2,0:T(8,128)(2,1)S(1)} async-done(((bf16[64,2,1,1,8,896]{5,4,1,3,2,0:T(8,128)(2,1)}), bf16[64,2,1,1,8,896]{5,4,1,3,2,0:T(8,128)(2,1)S(1)}, u32[]{:S(2)}, u32[]{:S(2)}) %all-to-all-start.1) | async-done | bytes 1835040 | tf_op jit(solution)/shard_map/all_to_all | solution.py:31
  78.9 8.5 %all-to-all-start.3 = ((s32[64,2,1,1,8]{4,1,3,2,0:T(2,128)}), s32[64,2,1,1,8]{4,1,3,2,0:T(2,128)S(1)}, u32[]{:S(2)}, u32[]{:S(2)}) async-start(s32[64,2,1,1,8]{4,1,3,2,0:T(2,128)} %copy.14), calls=%async_computation.3 | async-start | bytes 131072 | tf_op jit(solution)/shard_map/all_to_all | solution.py:31
  87.4 0.8 abs_reduce_fusion
  88.9 0.0 copy-done.3
  88.9 0.6 fusion.9
  90.3 9.4 %all-to-all-done.3 = s32[64,2,1,1,8]{4,1,3,2,0:T(2,128)S(1)} async-done(((s32[64,2,1,1,8]{4,1,3,2,0:T(2,128)}), s32[64,2,1,1,8]{4,1,3,2,0:T(2,128)S(1)}, u32[]{:S(2)}, u32[]{:S(2)}) %all-to-all-start.3) | async-done | bytes 4128 | tf_op jit(solution)/shard_map/all_to_all | solution.py:31
  99.7 3.0 %fusion.3 = s32[8,896]{1,0:T(8,128)S(1)} fusion(bf16[64,2,1,1,8,896]{5,4,1,3,2,0:T(8,128)(2,1)S(1)} %all-to-all-done.1, s32[64,2,8]{2,1,0:T(2,128)S(1)} %bitcast.26, f32[]{:T(128)} %bitcast.2), kind=kLoop, calls=%fused_computation.7 | loop fusion | flops 19260416 | bytes 1867780 | tf_op jit(solution)/shard_map/reduce_sum | solution.py:87
  102.8 12.0 %all-gather = f32[4,1,7169]{2,1,0:T(1,128)S(1)} all-gather(f32[1,1,7169]{2,1,0:T(1,128)S(1)} %maximum_bitcast_fusion), channel_id=1, replica_groups=mesh['dp_0'=8,'dp_1'=8,'dp_2'=2,'expert'=4] {'expert'}, dimensions={0}, use_global_device_ids=true | all-gather | bytes 143380 | tf_op jit(solution)/shard_map/all_gather | solution.py:44
  114.8 0.5 constant_dynamic-slice_fusion
  115.4 0.0 copy-done
  115.4 0.6 multiply_subtract_fusion
  (9 shorter events, 0.1 us)
Async XLA Ops:
  3.5 4.4 %copy-start.1 = (s32[1,1,1024]{2,1,0:T(1,128)S(1)}, s32[1,1,1024]{2,1,0:T(1,128)}, u32[]{:S(2)}) copy-start(s32[1,1,1024]{2,1,0:T(1,128)} %param.6) | copy-start | bytes 12292
  3.5 6.5 %all-to-all-start = ((bf16[64,2,1,1,8,896]{5,4,0,3,2,1:T(8,128)(2,1)}), bf16[64,2,1,1,8,896]{5,4,0,3,2,1:T(8,128)(2,1)S(1)}, u32[]{:S(2)}, u32[]{:S(2)}) async-start(bf16[64,2,1,1,8,896]{5,4,0,3,2,1:T(8,128)(2,1)} %copy.11), calls=%async_computation | async-start | bytes 3670016 | tf_op jit(solution)/shard_map/all_to_all | solution.py:31
  10.1 4.6 %all-to-all-start.2 = ((s32[2,1,512]{2,1,0:T(1,128)}), s32[2,1,512]{2,1,0:T(1,128)S(1)}, u32[]{:S(2)}, u32[]{:S(2)}) async-start(s32[2,1,512]{2,1,0:T(1,128)} %reshape.190), calls=%async_computation.2 | async-start | bytes 8192 | tf_op jit(solution)/shard_map/all_to_all | solution.py:31
  14.7 18.7 %copy-start.2 = (s32[4]{0:T(128)S(1)}, s32[4]{0:T(128)}, u32[]{:S(2)}) copy-start(s32[4]{0:T(128)} %param.7) | copy-start | bytes 52
  14.7 64.3 %all-to-all-start.1 = ((bf16[64,2,1,1,8,896]{5,4,1,3,2,0:T(8,128)(2,1)}), bf16[64,2,1,1,8,896]{5,4,1,3,2,0:T(8,128)(2,1)S(1)}, u32[]{:S(2)}, u32[]{:S(2)}) async-start(bf16[64,2,1,1,8,896]{5,4,1,3,2,0:T(8,128)(2,1)} %copy.12), calls=%async_computation.1 | async-start | bytes 3670016 | tf_op jit(solution)/shard_map/all_to_all | solution.py:31
  31.4 57.5 %copy-start.3 = (f32[60]{0:T(128)S(1)}, f32[60]{0:T(128)}, u32[]{:S(2)}) copy-start(f32[60]{0:T(128)} %constant.45.clone) | copy-start | bytes 724
  78.9 20.7 %all-to-all-start.3 = ((s32[64,2,1,1,8]{4,1,3,2,0:T(2,128)}), s32[64,2,1,1,8]{4,1,3,2,0:T(2,128)S(1)}, u32[]{:S(2)}, u32[]{:S(2)}) async-start(s32[64,2,1,1,8]{4,1,3,2,0:T(2,128)} %copy.14), calls=%async_computation.3 | async-start | bytes 131072 | tf_op jit(solution)/shard_map/all_to_all | solution.py:31
  88.3 27.1 %copy-start = (f32[1,8,896]{2,1,0:T(8,128)S(1)}, f32[1,8,896]{2,1,0:T(8,128)}, u32[]{:S(2)}) copy-start(f32[1,8,896]{2,1,0:T(8,128)} %param.8) | copy-start | bytes 86020
where the time goes:
time: 117 us; the launch traced here: 116 us
  waiting for transfers between devices  52.9 us (45%)
  starting transfers between devices  32.3 us (28%)
  blocking collectives  12 us (10%)
  local copies, waits for them, and re-layouts  7.64 us (7%)
  other arithmetic  7.13 us (6%)
  between operations  4.07 us (3%)
    all_to_all x4, waiting for transfers between devices, moved_by_axis(): lax.all_to_all(pieces, axes[k], split_axis=k, concat_axis=k, tiled=True)  52.9 us
    all_to_all x4, starting transfers between devices, moved_by_axis(): lax.all_to_all(pieces, axes[k], split_axis=k, concat_axis=k, tiled=True)  32.3 us
    all_gather x1, blocking collectives, in_one_piece(): out, at, outs = (lax.all_gather(both, axis, axis=dim, tiled=True), 0, [])  12 us
    another operation x3, local copies, waits for them, and re-layouts, moved_by_axis(): pieces = pieces.reshape(*shape, *pieces.shape[1:])  3.11 us
    reduce_sum x1, other arithmetic, body(): totals = jnp.sum(counts, axis=0, dtype=jnp.int32)  3.04 us
    all_to_all x3, local copies, waits for them, and re-layouts, moved_by_axis(): lax.all_to_all(pieces, axes[k], split_axis=k, concat_axis=k, tiled=True)  2.64 us
  transfers between devices with their start and end apart: 4, of which 3 were waited for; matrix products, arithmetic and copies ran while one was open for 7% of the time, Pallas kernels for 0%

commit v1 on v0

v1 whole, which is shorter than its diff:
```python
import jax
import jax.numpy as jnp
from jax import lax
from jax.experimental import pallas as pl
from jax.experimental.pallas import tpu as pltpu
from jax.sharding import Mesh
from jax.sharding import PartitionSpec as P

DP = ("dp_0", "dp_1", "dp_2")
MESH = pl.DeviceIdType.MESH
A = 8
X = 4
ROWS = 8
COLS = 896
TILES = COLS // 128
CHUNKS = 4
low_power = -30
high_power = 30
learn_rate = 0.05
HASH_MUL = 747796405
HASH_ADD = 1013904223
HASH_MIX = 1103515245


def order(k):
    return 4 + ((k + 1) // 2) * (2 * ((k + 1) % 2) - 1)


def kernel(
    g_hbm, off_ref, se_ref, mw_ref, mean_o, new_o, step_o,
    gv, rp, poff, pm, mxs, rm1, mxs2, rm2, inv_s, stp_s, ob, pb, sums, rc1, acc, rc2, xs, rx,
    ld, sd, rd, sm1, sr1, sm2, sr2, s1, r1, s2, r2, sx, rxs,
):
    z, y, c, x = (lax.axis_index(n) for n in ("dp_0", "dp_1", "dp_2", "expert"))
    a = y + c * (z - y)
    b = z + c * (y - z)

    def peer_a(ap):
        return (z + c * (ap - z), ap + c * (y - ap), c, x)

    def peer_b(bp):
        return (bp + c * (z - bp), y + c * (bp - y), c, x)

    def rdma(src, dst, send, recv, dev):
        return pltpu.make_async_remote_copy(
            src_ref=src, dst_ref=dst, send_sem=send, recv_sem=recv, device_id=dev, device_id_type=MESH
        )

    partner = (z, y, 1 - c, x)
    per = A * A // CHUNKS

    def load(q, h):
        rows = pl.ds(q * per, per)
        return pltpu.make_async_copy(g_hbm.at[rows, h], gv.at[h, rows], ld.at[q, h])

    for q in range(CHUNKS):
        for h in range(2):
            load(q, h).start()

    barrier = pltpu.get_barrier_semaphore()
    me16 = y * 2 + c

    def greet16(k, carry):
        p = (me16 + k) % (2 * A)
        pl.semaphore_signal(barrier, inc=1, device_id=(z, p // 2, p % 2, x), device_id_type=MESH)
        return carry

    def greet8(k, carry):
        pl.semaphore_signal(barrier, inc=1, device_id=((z + k) % A, y, c, x), device_id_type=MESH)
        return carry

    def greet4(k, carry):
        pl.semaphore_signal(barrier, inc=1, device_id=(z, y, c, (x + k) % X), device_id_type=MESH)
        return carry

    lax.fori_loop(1, 2 * A, greet16, 0)
    lax.fori_loop(1, A, greet8, 0)
    lax.fori_loop(1, X, greet4, 0)

    for q in range(CHUNKS):
        for h in range(2):
            load(q, h).wait()

            def block_max(i, carry):
                v = jnp.abs(gv[h, i].astype(jnp.float32))
                m = v[:, :128]
                for t in range(1, TILES):
                    m = jnp.maximum(m, v[:, t * 128 : (t + 1) * 128])
                pm[pl.ds((h * A * A + i) * ROWS, ROWS), :] = m
                return carry

            lax.fori_loop(q * per, (q + 1) * per, block_max, 0, unroll=2)
    top = pm[pl.ds(0, 128, stride=ROWS), :]
    for r in range(1, ROWS):
        top = jnp.maximum(top, pm[pl.ds(r, 128, stride=ROWS), :])
    mine = jnp.max(top.T, axis=0, keepdims=True)
    mxs[...] = mine
    rm1[me16] = mine

    pl.semaphore_wait(barrier, (2 * A - 1) + (A - 1) + (X - 1))

    def send_max(k, carry):
        p = (me16 + k) % (2 * A)
        rdma(mxs, rm1.at[me16], sm1.at[p], sr1.at[me16], (z, p // 2, p % 2, x)).start()
        return carry

    lax.fori_loop(1, 2 * A, send_max, 0)
    raw = rdma(gv.at[1 - c], rp, sd.at[0], rd.at[0], partner)
    raw_off = rdma(off_ref, poff, sd.at[1], rd.at[1], partner)
    raw_off.start()
    raw.start()

    def spread(ref, out):
        start = ref[...] * HASH_MUL + HASH_ADD
        for i in range(A):
            wide = jnp.broadcast_to(start[i : i + 1, :], (128, 128)).T
            out[pl.ds(i * 128, 128), :] = wide

    spread(off_ref, ob)

    def wait_max(k, carry):
        p = (me16 + k) % (2 * A)
        rdma(mxs, rm1.at[p], sm1.at[p], sr1.at[p], partner).wait_recv()
        return carry

    lax.fori_loop(1, 2 * A, wait_max, 0)
    ring = jnp.max(rm1[...], axis=0)
    mxs2[...] = ring
    rm2[z] = ring

    def send_max2(k, carry):
        p = (z + k) % A
        rdma(mxs2, rm2.at[z], sm2.at[p], sr2.at[z], (p, y, c, x)).start()
        return carry

    lax.fori_loop(1, A, send_max2, 0)
    raw_off.wait_recv()
    spread(poff, pb)

    def wait_max2(k, carry):
        p = (z + k) % A
        rdma(mxs2, rm2.at[p], sm2.at[p], sr2.at[p], partner).wait_recv()
        return carry

    lax.fori_loop(1, A, wait_max2, 0)
    best = jnp.max(rm2[...], axis=0)
    step = jnp.full((1, 128), 2.0 ** (low_power - 6), jnp.float32)
    inverse = jnp.full((1, 128), 2.0 ** (6 - low_power + 20), jnp.float32)
    for e in range(low_power, high_power):
        over = best >= 2.0**e
        step = jnp.where(over, jnp.float32(2.0 ** (e - 5)), step)
        inverse = jnp.where(over, jnp.float32(2.0 ** (25 - e)), inverse)
    inv_s[...] = jnp.broadcast_to(inverse, (128, 128)).T
    stp_s[...] = jnp.broadcast_to(step, (128, 128)).T

    lane = lax.broadcasted_iota(jnp.int32, (ROWS, 128), 1)
    column = [(lane + t * 128) * HASH_MUL for t in range(TILES)]
    raw.wait_recv()

    def rounded(tile, inverse, noise):
        whole = jnp.floor(tile.astype(jnp.float32) * inverse).astype(jnp.int32)
        noise = noise ^ (noise >> 13)
        noise = noise * HASH_MIX
        noise = noise ^ (noise >> 16)
        return (whole + (noise & 0xFF000)) >> 20

    def first_send(ap):
        return rdma(sums.at[ap], rc1.at[a], s1.at[ap], r1.at[a], peer_a(ap))

    def quantize_chunk(ap):
        def one(bp, carry):
            zy = ap * (1 + 7 * c) + bp * (8 - 7 * c)
            inverse = jnp.broadcast_to(inv_s[pl.ds(c * A * A + zy, 1), :], (ROWS, 128))
            rows = pl.ds((zy * 2 + c) * ROWS, ROWS)
            mine, theirs = ob[rows, :], pb[rows, :]
            for t in range(TILES):
                cols = pl.ds(t * 128, 128)
                both = rounded(gv[c, zy, :, cols], inverse, mine + column[t])
                both += rounded(rp[zy, :, cols], inverse, theirs + column[t])
                sums[ap, bp, :, cols] = both.astype(jnp.float32).astype(jnp.bfloat16)
            return carry

        lax.fori_loop(0, A, one, 0)

    def quantize_send(k, carry):
        ap = (a + order(k)) % A
        quantize_chunk(ap)
        first_send(ap).start()
        return carry

    lax.fori_loop(0, A - 1, quantize_send, 0)
    quantize_chunk(a)

    def clear(bp, carry):
        acc[bp] = sums[a, bp].astype(jnp.float32)
        return carry

    lax.fori_loop(0, A, clear, 0)

    def gather_first(k, carry):
        ap = (a - order(k) + A) % A
        rdma(sums.at[0], rc1.at[ap], s1.at[ap], r1.at[ap], partner).wait_recv()

        def add(bp, inner):
            acc[bp] += rc1[ap, bp].astype(jnp.float32)
            return inner

        lax.fori_loop(0, A, add, 0)
        return carry

    lax.fori_loop(0, A - 1, gather_first, 0)

    def second_send(k, carry):
        bp = (b + order(k)) % A
        rdma(acc.at[bp], rc2.at[b], s2.at[bp], r2.at[b], peer_b(bp)).start()
        return carry

    lax.fori_loop(0, A - 1, second_send, 0)
    rc2[b] = acc[b]

    def gather_second(k, carry):
        bp = (b - order(k) + A) % A
        rdma(acc.at[0], rc2.at[bp], s2.at[bp], r2.at[bp], partner).wait_recv()
        return carry

    lax.fori_loop(0, A - 1, gather_second, 0)
    own = stp_s[pl.ds(c * A * A + z * A + y, 1), :]
    total = rc2[0]
    for i in range(1, A):
        total += rc2[i]
    own8 = jnp.broadcast_to(own, (ROWS, 128))
    share = own8 * (1.0 / (2 * A * A))
    for t in range(TILES):
        xs[:, t * 128 : (t + 1) * 128] = total[:, t * 128 : (t + 1) * 128] * share
    xs[:, COLS:] = own8

    def send_x(k, carry):
        xp = (x + k) % X
        rdma(xs, rx.at[x], sx.at[xp], rxs.at[x], (z, y, c, xp)).start()
        return carry

    lax.fori_loop(1, X, send_x, 0)
    rx[x] = xs[...]

    def wait_x(k, carry):
        xp = (x + k) % X
        rdma(xs, rx.at[xp], sx.at[xp], rxs.at[xp], partner).wait_recv()
        return carry

    lax.fori_loop(1, X, wait_x, 0)
    value = rx[X - 1]
    for s in range(X - 1):
        value = jnp.where(se_ref[s] == x, rx[s], value)
    mean = value[:, :COLS]
    mean_o[...] = mean
    new_o[...] = mw_ref[...] - learn_rate * mean
    step_o[...] = value[0:1, COLS : COLS + 1]

    raw.wait_send()
    raw_off.wait_send()

    def drain16(k, carry):
        p = (me16 + k) % (2 * A)
        rdma(mxs, rm1.at[me16], sm1.at[p], sr1.at[me16], partner).wait_send()
        return carry

    lax.fori_loop(1, 2 * A, drain16, 0)

    def drain8(k, carry):
        rdma(mxs2, rm2.at[z], sm2.at[(z + k) % A], sr2.at[z], partner).wait_send()
        rdma(sums.at[0], rc1.at[a], s1.at[(a + k) % A], r1.at[a], partner).wait_send()
        rdma(acc.at[0], rc2.at[b], s2.at[(b + k) % A], r2.at[b], partner).wait_send()
        return carry

    lax.fori_loop(1, A, drain8, 0)

    def drain4(k, carry):
        rdma(xs, rx.at[x], sx.at[(x + k) % X], rxs.at[x], partner).wait_send()
        return carry

    lax.fori_loop(1, X, drain4, 0)


def body(expert_grads, round_offsets, slot_expert, master_weight):
    n = A * A
    f32, bf16, i32 = jnp.float32, jnp.bfloat16, jnp.int32
    dma = pltpu.SemaphoreType.DMA
    vmem = pl.BlockSpec(memory_space=pltpu.VMEM)
    mean, new, step = pl.pallas_call(
        kernel,
        name="average",
        out_shape=(
            jax.ShapeDtypeStruct((ROWS, COLS), f32),
            jax.ShapeDtypeStruct((ROWS, COLS), f32),
            jax.ShapeDtypeStruct((1, 1), f32),
        ),
        in_specs=[
            pl.BlockSpec(memory_space=pl.ANY),
            vmem,
            pl.BlockSpec(memory_space=pltpu.SMEM),
            vmem,
        ],
        out_specs=(vmem, vmem, vmem),
        scratch_shapes=[
            pltpu.VMEM((2, n, ROWS, COLS), bf16),
            pltpu.VMEM((n, ROWS, COLS), bf16),
            pltpu.VMEM((A, 128), i32),
            pltpu.VMEM((2 * n * ROWS, 128), f32),
            pltpu.VMEM((1, 128), f32),
            pltpu.VMEM((2 * A, 1, 128), f32),
            pltpu.VMEM((1, 128), f32),
            pltpu.VMEM((A, 1, 128), f32),
            pltpu.VMEM((128, 128), f32),
            pltpu.VMEM((128, 128), f32),
            pltpu.VMEM((2 * n * ROWS, 128), i32),
            pltpu.VMEM((2 * n * ROWS, 128), i32),
            pltpu.VMEM((A, A, ROWS, COLS), bf16),
            pltpu.VMEM((A, A, ROWS, COLS), bf16),
            pltpu.VMEM((A, ROWS, COLS), f32),
            pltpu.VMEM((A, ROWS, COLS), f32),
            pltpu.VMEM((ROWS, COLS + 128), f32),
            pltpu.VMEM((X, ROWS, COLS + 128), f32),
            dma((CHUNKS, 2)),
            dma((2,)),
            dma((2,)),
            dma((2 * A,)),
            dma((2 * A,)),
            dma((A,)),
            dma((A,)),
            dma((A,)),
            dma((A,)),
            dma((A,)),
            dma((A,)),
            dma((X,)),
            dma((X,)),
        ],
        compiler_params=pltpu.CompilerParams(collective_id=0, has_side_effects=True),
    )(
        expert_grads.reshape(n, 2, ROWS, COLS),
        round_offsets.reshape(A, 128),
        slot_expert,
        master_weight.reshape(ROWS, COLS),
    )
    return mean[None], new[None], step


def solution(mesh):
    finer = Mesh(
        mesh.devices.reshape(A, A, 2, mesh.shape["expert"]), ("dp_0", "dp_1", "dp_2", "expert")
    )
    return jax.shard_map(
        body,
        mesh=finer,
        in_specs=(P(DP, "expert", None, None), P(DP, "expert", None), P(), P("expert", DP, None)),
        out_specs=(P("expert", DP, None), P("expert", DP, None), P("expert", DP)),
        check_vma=False,
    )
```

time: 117 us -> 55.1 us (0.47)
  the two profiles are of different devices: /device:TPU:6 before, /device:TPU:8 now
where the time goes in v1:
time: 55.1 us; the launch traced here: 54.7 us
  Pallas kernels  49.6 us (90%)
  local copies, waits for them, and re-layouts  2.72 us (5%)
  between operations  2.39 us (4%)
    pallas_call x1, Pallas kernels, body(): pl.pallas_call(kernel, name='average', out_shape=(jax.ShapeDtypeStruct((R...  49.6 us
    unnamed x2, local copies, waits for them, and re-layouts  2.72 us

profile of v1, /device:TPU:8, one launch (start us, length us, event | category | flops | bytes accessed | tf_op | source)
XLA Modules:
  0.0 54.7 jit_solution(10237403174874904922)
XLA Ops:
  0.6 49.6 %average.1 = (f32[8,896]{1,0:T(8,128)}, f32[8,896]{1,0:T(8,128)}, f32[1,1]{1,0:T(1,128)}) custom-call(bf16[64,2,8,896]{3,2,1,0:T(8,128)(2,1)} %bitcast.5, s32[8,128]{1,0:T(8,128)} %bitcast.9, s32[4]{0:T(128)} %se_ref.1, f32[8,896]{1,0:T(8,128)} %bitcast.6), custom_call_target="tpu_custom_call" | custom-call | tf_op jit(solution)/shard_map/average/pallas_call | solution.py:289
  50.3 1.4 %copy.10 = f32[1,8,896]{2,1,0:T(8,128)} copy(f32[1,8,896]{2,1,0:T(8,128)} %bitcast.8) | data formatting | bytes 57344
  51.6 1.4 %copy.11 = f32[1,8,896]{2,1,0:T(8,128)} copy(f32[1,8,896]{2,1,0:T(8,128)} %bitcast.7) | data formatting | bytes 57344

commit v2 on v1

v2 whole, which is shorter than its diff:
```python
import jax
import jax.numpy as jnp
from jax import lax
from jax.experimental import pallas as pl
from jax.experimental.pallas import tpu as pltpu
from jax.sharding import Mesh
from jax.sharding import PartitionSpec as P

DP = ("dp_0", "dp_1", "dp_2")
MESH = pl.DeviceIdType.MESH
A = 8
X = 4
H = A // 2
ROWS = 8
COLS = 896
TILES = COLS // 128
CHUNKS = 4
low_power = -30
high_power = 30
learn_rate = 0.05
HASH_MUL = 747796405
HASH_ADD = 1013904223
HASH_MIX = 1103515245


def order(k):
    return 4 + ((k + 1) // 2) * (2 * ((k + 1) % 2) - 1)


def kernel(
    g_hbm, off_hbm, rx,
    gv, rp, offv, roff, toff, obs, pm, mxs, rm1, mxs2, rm2, inv_s, stp_s, sums, rc1, acc, rc2,
    ld, lo, so, ro, sraw, rr, sm1, sr1, sm2, sr2, s1, r1, s2, r2, sx, rxs,
):
    z, y, c, x = (lax.axis_index(n) for n in ("dp_0", "dp_1", "dp_2", "expert"))
    a = y + c * (z - y)
    b = z + c * (y - z)

    def peer_a(ap):
        return (z + c * (ap - z), ap + c * (y - ap), c, x)

    def peer_b(bp):
        return (bp + c * (z - bp), y + c * (bp - y), c, x)

    def rdma(src, dst, send, recv, dev):
        return pltpu.make_async_remote_copy(
            src_ref=src, dst_ref=dst, send_sem=send, recv_sem=recv, device_id=dev, device_id_type=MESH
        )

    partner = (z, y, 1 - c, x)
    per = A // CHUNKS

    def way(position, h):
        return 2 * ((position + h) & 1) - 1

    def load(q, h):
        rows = pl.ds(q * per, per)
        return pltpu.make_async_copy(g_hbm.at[rows, :, h], gv.at[h, rows], ld.at[q, h])

    load_off = pltpu.make_async_copy(off_hbm, offv, lo.at[0])
    load_off.start()
    for q in range(CHUNKS):
        for h in range(2):
            load(q, h).start()

    barrier = pltpu.get_barrier_semaphore()
    me16 = y * 2 + c

    def greet(dev):
        pl.semaphore_signal(barrier, inc=1, device_id=dev, device_id_type=MESH)

    def greet16(k, carry):
        p = (me16 + k) & 15
        greet((z, p >> 1, p & 1, x))
        return carry

    def greet8(k, carry):
        greet(((z + k) & 7, y, c, x))
        return carry

    def greet4(k, carry):
        greet((z, y, c, (x + k) & 3))
        return carry

    lax.fori_loop(1, 2 * A, greet16, 0)
    lax.fori_loop(1, A, greet8, 0)
    lax.fori_loop(1, X, greet4, 0)
    greet(((z + 1) & 7, y, 1 - c, x))
    greet(((z + 7) & 7, y, 1 - c, x))

    for q in range(CHUNKS):
        for h in range(2):
            load(q, h).wait()

            def block_max(i, carry):
                v = jnp.abs(gv[h, i >> 3, i & 7].astype(jnp.float32))
                m = v[:, :128]
                for t in range(1, TILES):
                    m = jnp.maximum(m, v[:, t * 128 : (t + 1) * 128])
                pm[pl.ds((h * A * A + i) * ROWS, ROWS), :] = m
                return carry

            lax.fori_loop(q * per * A, (q + 1) * per * A, block_max, 0, unroll=4)
    top = pm[pl.ds(0, 128, stride=ROWS), :]
    for r in range(1, ROWS):
        top = jnp.maximum(top, pm[pl.ds(r, 128, stride=ROWS), :])
    mine = jnp.max(top.T, axis=0, keepdims=True)
    mxs[...] = mine
    rm1[me16] = mine
    load_off.wait()

    pl.semaphore_wait(barrier, (2 * A - 1) + (A - 1) + (X - 1) + 2)

    def send_max(k, carry):
        p = (me16 + k) & 15
        rdma(mxs, rm1.at[me16], sm1.at[p], sr1.at[me16], (z, p >> 1, p & 1, x)).start()
        return carry

    lax.fori_loop(1, 2 * A, send_max, 0)

    halves = [pl.ds(h * H, H) for h in range(2)]

    def raw_rows(core, position, h):
        return gv.at[core, halves[h], position] if core == 0 else gv.at[core, position, halves[h]]

    rdma(offv, roff.at[0], so.at[0], ro.at[0], partner).start()
    for core, position in ((0, y), (1, z)):
        for h in range(2):
            near = (position - way(position, h)) & 7
            dev = (z, near, 0, x) if core == 0 else (near, y, 1, x)
            slot = 1 + 2 * h + c
            rdma(offv, roff.at[slot], so.at[1 + 2 * core + h], ro.at[slot], dev).start()
            for m in range(H):
                dest = (position - way(position, h) * (1 + m)) & 7
                rdma(
                    raw_rows(core, dest, h), rp.at[1 + c, m, halves[h]], sraw.at[core, h, m], rr.at[1 + c, h, m], dev
                ).start()

        @pl.when(c != core)
        def _():
            for h in range(2):
                for m in range(H):
                    dest = (position + way(position, h) * m) & 7
                    rdma(
                        raw_rows(core, dest, h), rp.at[0, m, halves[h]], sraw.at[2, h, m], rr.at[0, h, m], partner
                    ).start()

    def turned(value, slot):
        start = value * HASH_MUL + HASH_ADD
        toff[slot] = jnp.concatenate([start] * 16, axis=0).T

    def block_of(m, bp, h):
        ap = (a + way(a, h) * m) & 7
        return bp + c * (ap - bp), ap + c * (bp - ap)

    def spread(which, slots):
        for m in range(H):
            for bp in range(A):
                zp, yp = block_of(m, bp, bp // H)
                tile = toff[slots[bp // H], pl.ds((yp * 2 + c) * ROWS, ROWS), :]
                index = jnp.full((ROWS, 128), zp, jnp.int32)
                obs[which, m, bp] = jnp.take_along_axis(tile, index, axis=1, mode="promise_in_bounds")

    turned(offv[...], 5)
    spread(0, (5, 5))

    def wait_max(k, carry):
        p = (me16 + k) & 15
        rdma(mxs, rm1.at[p], sm1.at[p], sr1.at[p], partner).wait_recv()
        return carry

    lax.fori_loop(1, 2 * A, wait_max, 0)
    ring = jnp.max(rm1[...], axis=0)
    mxs2[...] = ring
    rm2[z] = ring

    def send_max2(k, carry):
        p = (z + k) & 7
        rdma(mxs2, rm2.at[z], sm2.at[p], sr2.at[z], (p, y, c, x)).start()
        return carry

    lax.fori_loop(1, A, send_max2, 0)
    for i in range(5):
        rdma(offv, roff.at[i], so.at[0], ro.at[i], partner).wait_recv()
        turned(roff[i], i)
    spread(1, (0, 0))
    spread(2, (1, 3))
    spread(3, (2, 4))

    def wait_max2(k, carry):
        p = (z + k) & 7
        rdma(mxs2, rm2.at[p], sm2.at[p], sr2.at[p], partner).wait_recv()
        return carry

    lax.fori_loop(1, A, wait_max2, 0)
    best = jnp.broadcast_to(jnp.max(rm2[...], axis=0), (ROWS, 128))
    step = jnp.full((ROWS, 128), 2.0 ** (low_power - 6), jnp.float32)
    inverse = jnp.full((ROWS, 128), 2.0 ** (6 - low_power + 20), jnp.float32)
    for e in range(low_power, high_power):
        over = best >= 2.0**e
        step = jnp.where(over, jnp.float32(2.0 ** (e - 5)), step)
        inverse = jnp.where(over, jnp.float32(2.0 ** (25 - e)), inverse)
    inv_s[...] = inverse
    stp_s[...] = step

    lane = lax.broadcasted_iota(jnp.int32, (ROWS, 128), 1)
    column = [(lane + t * 128) * HASH_MUL for t in range(TILES)]

    def rounded(tile, scale, noise):
        whole = jnp.floor(tile.astype(jnp.float32) * scale).astype(jnp.int32)
        noise = noise ^ (noise >> 13)
        noise = noise * HASH_MIX
        noise = noise ^ (noise >> 16)
        return (whole + (noise & 0xFF000)) >> 20

    def pick(ref, block):
        index = jnp.full((ROWS, 128), block, jnp.int32)
        return jnp.take_along_axis(ref[...], index, axis=1, mode="promise_in_bounds")

    def first_send(h, m):
        half = halves[h]
        return rdma(
            sums.at[m, half], rc1.at[m - 1, half], s1.at[h, m - 1], r1.at[h, m - 1], peer_a((a + way(a, h) * m) & 7)
        )

    for m in range(H - 1, -1, -1):
        for h in range(2):
            for j in range(3):
                rdma(rp.at[j, m, halves[h]], rp.at[j, m, halves[h]], sraw.at[0, h, m], rr.at[j, h, m], partner).wait_recv()

            def one(bp, carry):
                zp, yp = block_of(m, bp, h)
                scale = pick(inv_s, c * A * A + zp * A + yp)
                starts = [obs[j, m, bp] for j in range(4)]
                for t in range(TILES):
                    cols = pl.ds(t * 128, 128)
                    both = rounded(gv[c, zp, yp, :, cols], scale, starts[0] + column[t])
                    for j in range(3):
                        both += rounded(rp[j, m, bp, :, cols], scale, starts[1 + j] + column[t])
                    sums[m, bp, :, cols] = both.astype(jnp.float32).astype(jnp.bfloat16)
                return carry

            lax.fori_loop(h * H, (h + 1) * H, one, 0)
            if m:
                first_send(h, m).start()

    for h in range(2):
        for m in range(1, H):
            first_send(h, m).wait_recv()

        def add(bp, carry):
            total = sums[0, bp].astype(jnp.float32)
            for m in range(H - 1):
                total += rc1[m, bp].astype(jnp.float32)
            acc[bp] = total

            @pl.when(bp != b)
            def _():
                rdma(acc.at[bp], rc2.at[b], s2.at[bp], r2.at[b], peer_b(bp)).start()

            return carry

        lax.fori_loop(h * H, (h + 1) * H, add, 0)
    rc2[b] = acc[b]
    own = pick(stp_s, c * A * A + z * A + y)

    def gather_second(k, carry):
        bp = (b + k) & 7
        rdma(acc.at[bp], rc2.at[bp], s2.at[bp], r2.at[bp], partner).wait_recv()
        return carry

    lax.fori_loop(1, A, gather_second, 0)
    total = rc2[0]
    for i in range(1, A):
        total += rc2[i]
    share = own * (1.0 / (2 * A * A))
    for t in range(TILES):
        rx[x, :, t * 128 : (t + 1) * 128] = total[:, t * 128 : (t + 1) * 128] * share
    rx[x, :, COLS:] = own

    def send_x(k, carry):
        xp = (x + k) & 3
        rdma(rx.at[x], rx.at[x], sx.at[xp], rxs.at[x], (z, y, c, xp)).start()
        return carry

    lax.fori_loop(1, X, send_x, 0)

    for i in range(5):
        rdma(offv, roff.at[i], so.at[i], ro.at[i], partner).wait_send()
    for j in range(3):
        for h in range(2):
            for m in range(H):
                rdma(rp.at[j, m, halves[h]], rp.at[j, m, halves[h]], sraw.at[j, h, m], rr.at[j, h, m], partner).wait_send()
    for h in range(2):
        for m in range(1, H):
            first_send(h, m).wait_send()

    def drain16(k, carry):
        p = (me16 + k) & 15
        rdma(mxs, rm1.at[me16], sm1.at[p], sr1.at[me16], partner).wait_send()
        return carry

    lax.fori_loop(1, 2 * A, drain16, 0)

    def drain8(k, carry):
        rdma(mxs2, rm2.at[z], sm2.at[(z + k) & 7], sr2.at[z], partner).wait_send()
        bp = (b + k) & 7
        rdma(acc.at[bp], rc2.at[b], s2.at[bp], r2.at[b], partner).wait_send()
        return carry

    lax.fori_loop(1, A, drain8, 0)

    def wait_x(k, carry):
        xp = (x + k) & 3
        rdma(rx.at[xp], rx.at[xp], sx.at[xp], rxs.at[xp], partner).wait_recv()
        return carry

    lax.fori_loop(1, X, wait_x, 0)

    def drain4(k, carry):
        xp = (x + k) & 3
        rdma(rx.at[x], rx.at[x], sx.at[xp], rxs.at[x], partner).wait_send()
        return carry

    lax.fori_loop(1, X, drain4, 0)


def finish(rx, se_ref, mw_ref, mean_o, new_o, step_o):
    x = lax.axis_index("expert")
    value = rx[X - 1]
    for s in range(X - 1):
        value = jnp.where(se_ref[s] == x, rx[s], value)
    mean = value[:, :COLS]
    mean_o[...] = mean
    new_o[...] = mw_ref[...] - learn_rate * mean
    step_o[...] = value[0:1, COLS : COLS + 1]


def body(expert_grads, round_offsets, slot_expert, master_weight):
    f32, bf16, i32 = jnp.float32, jnp.bfloat16, jnp.int32
    dma = pltpu.SemaphoreType.DMA
    vmem = pl.BlockSpec(memory_space=pltpu.VMEM)
    hbm = pl.BlockSpec(memory_space=pl.ANY)
    gathered = pl.pallas_call(
        kernel,
        name="average",
        out_shape=pltpu.VMEM((X, ROWS, COLS + 128), f32),
        in_specs=[hbm, hbm],
        out_specs=vmem,
        scratch_shapes=[
            pltpu.VMEM((2, A, A, ROWS, COLS), bf16),
            pltpu.VMEM((3, H, A, ROWS, COLS), bf16),
            pltpu.VMEM((A, 128), i32),
            pltpu.VMEM((5, A, 128), i32),
            pltpu.VMEM((6, 128, 128), i32),
            pltpu.VMEM((4, H, A, ROWS, 128), i32),
            pltpu.VMEM((2 * A * A * ROWS, 128), f32),
            pltpu.VMEM((1, 128), f32),
            pltpu.VMEM((2 * A, 1, 128), f32),
            pltpu.VMEM((1, 128), f32),
            pltpu.VMEM((A, 1, 128), f32),
            pltpu.VMEM((ROWS, 128), f32),
            pltpu.VMEM((ROWS, 128), f32),
            pltpu.VMEM((H, A, ROWS, COLS), bf16),
            pltpu.VMEM((H - 1, A, ROWS, COLS), bf16),
            pltpu.VMEM((A, ROWS, COLS), f32),
            pltpu.VMEM((A, ROWS, COLS), f32),
            dma((CHUNKS, 2)),
            dma((1,)),
            dma((5,)),
            dma((5,)),
            dma((3, 2, H)),
            dma((3, 2, H)),
            dma((2 * A,)),
            dma((2 * A,)),
            dma((A,)),
            dma((A,)),
            dma((2, H - 1)),
            dma((2, H - 1)),
            dma((A,)),
            dma((A,)),
            dma((X,)),
            dma((X,)),
        ],
        compiler_params=pltpu.CompilerParams(collective_id=0, has_side_effects=True),
    )(expert_grads.reshape(A, A, 2, ROWS, COLS), round_offsets.reshape(A, 128))
    mean, new, step = pl.pallas_call(
        finish,
        name="finish",
        out_shape=(
            jax.ShapeDtypeStruct((ROWS, COLS), f32),
            jax.ShapeDtypeStruct((ROWS, COLS), f32),
            jax.ShapeDtypeStruct((1, 1), f32),
        ),
        in_specs=[vmem, pl.BlockSpec(memory_space=pltpu.SMEM), vmem],
        out_specs=(vmem, vmem, vmem),
        compiler_params=pltpu.CompilerParams(vmem_limit_bytes=1024 * 1024),
    )(gathered, slot_expert, master_weight.reshape(ROWS, COLS))
    return mean[None], new[None], step


def solution(mesh):
    finer = Mesh(
        mesh.devices.reshape(A, A, 2, mesh.shape["expert"]), ("dp_0", "dp_1", "dp_2", "expert")
    )
    return jax.shard_map(
        body,
        mesh=finer,
        in_specs=(P(DP, "expert", None, None), P(DP, "expert", None), P(), P("expert", DP, None)),
        out_specs=(P("expert", DP, None), P("expert", DP, None), P("expert", DP)),
        check_vma=False,
    )
```

time: 55.1 us -> 42.8 us (0.78)
  the two profiles are of different devices: /device:TPU:8 before, /device:TPU:64 now
where the time goes in v2:
time: 42.8 us; the launch traced here: 42.6 us
  Pallas kernels  41.9 us (98%)
  between operations  0.67 us (2%)
    pallas_call x1, Pallas kernels, body(): pl.pallas_call(kernel, name='average', out_shape=pltpu.VMEM((X, ROWS, COL...  40.8 us
    pallas_call x1, Pallas kernels, body(): pl.pallas_call(finish, name='finish', out_shape=(jax.ShapeDtypeStruct((RO...  1.18 us

profile of v2, /device:TPU:64, one launch (start us, length us, event | category | flops | bytes accessed | tf_op | source)
XLA Modules:
  0.0 42.6 jit_solution(3498982229739024029)
XLA Ops:
  0.6 0.0 copy-start
  0.6 0.0 copy-start.1
  0.7 40.8 %average.1.rx = f32[4,8,1024]{2,1,0:T(8,128)S(1)} custom-call(bf16[8,8,2,8,896]{4,3,2,1,0:T(8,128)(2,1)} %bitcast.6, s32[8,128]{1,0:T(8,128)} %bitcast.7), custom_call_target="tpu_custom_call" | custom-call | tf_op jit(solution)/shard_map/average/pallas_call | solution.py:344
  41.4 0.0 copy-done
  41.4 0.0 copy-done.1
  41.4 1.2 %finish.1 = (f32[8,896]{1,0:T(8,128)}, f32[8,896]{1,0:T(8,128)}, f32[1,1]{1,0:T(1,128)}) custom-call(f32[4,8,1024]{2,1,0:T(8,128)S(1)} %average.1.rx, s32[4]{0:T(128)S(1)} %copy-done.1, f32[8,896]{1,0:T(8,128)S(1)} %bitcast.5), custom_call_target="tpu_custom_call" | custom-call | tf_op jit(solution)/shard_map/finish/pallas_call | solution.py:387
Async XLA Ops:
  0.6 40.8 %copy-start = (f32[1,8,896]{2,1,0:T(8,128)S(1)}, f32[1,8,896]{2,1,0:T(8,128)}, u32[]{:S(2)}) copy-start(f32[1,8,896]{2,1,0:T(8,128)} %param.7) | copy-start | bytes 86020
  0.6 40.8 %copy-start.1 = (s32[4]{0:T(128)S(1)}, s32[4]{0:T(128)}, u32[]{:S(2)}) copy-start(s32[4]{0:T(128)} %se_ref.1) | copy-start | bytes 52

commit v3 on v2

v3 whole, which is shorter than its diff:
```python
import jax
import jax.numpy as jnp
from jax import lax
from jax.experimental import pallas as pl
from jax.experimental.pallas import tpu as pltpu
from jax.sharding import Mesh
from jax.sharding import PartitionSpec as P

DP = ("dp_0", "dp_1", "dp_2")
MESH = pl.DeviceIdType.MESH
A = 8
X = 4
H = A // 2
ROWS = 8
COLS = 896
TILES = COLS // 128
CHUNKS = 4
low_power = -30
high_power = 30
learn_rate = 0.05
HASH_MUL = 747796405
HASH_ADD = 1013904223
HASH_MIX = 1103515245


def kernel(
    g_hbm, off_hbm, rx,
    gv, rp, offv, roff, toff, noise, pm, mxs, rm1, mxs2, rm2, stp_s, scl, sums, rc,
    ld, lo, so, ro, sraw, rr, sm1, sr1, sm2, sr2, s1, r1, sx, rxs,
):
    z, y, c, x = (lax.axis_index(n) for n in ("dp_0", "dp_1", "dp_2", "expert"))

    def rdma(src, dst, send, recv, dev):
        return pltpu.make_async_remote_copy(
            src_ref=src, dst_ref=dst, send_sem=send, recv_sem=recv, device_id=dev, device_id_type=MESH
        )

    partner = (z, y, 1 - c, x)
    per = A // CHUNKS

    def way(position, core):
        return 2 * ((position + core) & 1) - 1

    def load(q, h):
        rows = pl.ds(q * per, per)
        return pltpu.make_async_copy(g_hbm.at[rows, :, h], gv.at[h, rows], ld.at[q, h])

    load_off = pltpu.make_async_copy(off_hbm, offv, lo.at[0])
    load_off.start()
    for q in range(CHUNKS):
        for h in range(2):
            load(q, h).start()

    barrier = pltpu.get_barrier_semaphore()
    me16 = y * 2 + c
    mz16 = z * 2 + c

    def greet(dev):
        pl.semaphore_signal(barrier, inc=1, device_id=dev, device_id_type=MESH)

    def greet16(k, carry):
        p = (me16 + k) & 15
        greet((z, p >> 1, p & 1, x))
        return carry

    def greet14(k, carry):
        p = (mz16 + k) & 15

        @pl.when((p >> 1) != z)
        def _():
            greet((p >> 1, y, p & 1, x))

        return carry

    def greet4(k, carry):
        greet((z, y, c, (x + k) & 3))
        return carry

    def near(position, core):
        return (position - way(position, core)) & 7

    lax.fori_loop(1, 2 * A, greet16, 0)
    lax.fori_loop(1, 2 * A, greet14, 0)
    lax.fori_loop(1, X, greet4, 0)
    greet((near(z, c), near(y, c), c, x))
    greet((near(z, c), near(y, c), 1 - c, x))
    greet((near(z, 1 - c), near(y, 1 - c), 1 - c, x))

    for q in range(CHUNKS):
        for h in range(2):
            load(q, h).wait()

            def block_max(i, carry):
                v = jnp.abs(gv[h, i >> 3, i & 7].astype(jnp.float32))
                m = v[:, :128]
                for t in range(1, TILES):
                    m = jnp.maximum(m, v[:, t * 128 : (t + 1) * 128])
                pm[pl.ds((h * A * A + i) * ROWS, ROWS), :] = m
                return carry

            lax.fori_loop(q * per * A, (q + 1) * per * A, block_max, 0, unroll=4)
    top = pm[pl.ds(0, 128, stride=ROWS), :]
    for r in range(1, ROWS):
        top = jnp.maximum(top, pm[pl.ds(r, 128, stride=ROWS), :])
    mine = jnp.max(top.T, axis=0, keepdims=True)
    mxs[...] = mine
    rm1[me16] = mine
    load_off.wait()

    pl.semaphore_wait(barrier, (2 * A - 1) + (2 * A - 2) + (X - 1) + 3)

    def send_max(k, carry):
        p = (me16 + k) & 15
        rdma(mxs, rm1.at[me16], sm1.at[p], sr1.at[me16], (z, p >> 1, p & 1, x)).start()
        return carry

    lax.fori_loop(1, 2 * A, send_max, 0)

    def to_near(core, q):
        return (near(z, core) if q else z, y if q == 1 else near(y, core), core, x)

    def dest(position, core, away, m):
        return (position + way(position, core) * ((-1 - m) if away else m)) & 7

    rdma(offv, roff.at[0], so.at[0], ro.at[0], partner).start()
    for core in range(2):
        for q in range(3):
            slot = 1 + 2 * q + c
            rdma(offv, roff.at[slot], so.at[1 + 3 * core + q], ro.at[slot], to_near(core, q)).start()

    def raw_part(first):
        def one(i, carry):
            mz, my = (i >> 2), i & 3
            for core in range(2):
                for q in (2, 1, 0):
                    src = gv.at[core, dest(z, core, q > 0, mz), dest(y, core, q != 1, my)]
                    slot = 1 + 2 * q + c
                    rdma(src, rp.at[slot, mz, my], sraw.at[3 * core + q], rr.at[slot, mz], to_near(core, q)).start()
            src = gv.at[1 - c, dest(z, 1 - c, False, mz), dest(y, 1 - c, False, my)]
            rdma(src, rp.at[0, mz, my], sraw.at[6], rr.at[0, mz], partner).start()
            return carry

        lax.fori_loop(first, first + 2 * H, one, 0)

    raw_part(2 * H)

    lane = lax.broadcasted_iota(jnp.int32, (ROWS, 128), 1)
    column = [(lane + t * 128) * HASH_MUL for t in range(TILES)]

    def dither(j, value):
        start = value * HASH_MUL + HASH_ADD
        toff[j] = jnp.concatenate([start] * 16, axis=0).T

        def one(mz, carry):
            zp = dest(z, c, False, mz)
            index = jnp.full((ROWS, 128), zp, jnp.int32)
            for my in range(H):
                yp = dest(y, c, False, my)
                tile = toff[j, pl.ds((yp * 2 + c) * ROWS, ROWS), :]
                code = jnp.take_along_axis(tile, index, axis=1, mode="promise_in_bounds")
                for t in range(TILES):
                    v = code + column[t]
                    v = v ^ (v >> 13)
                    v = v * HASH_MIX
                    v = v ^ (v >> 16)
                    noise[j, mz, my, :, pl.ds(t * 128, 128)] = v & 0xFF000
            return carry

        lax.fori_loop(0, H, one, 0)

    dither(7, offv[...])

    def wait_max(k, carry):
        p = (me16 + k) & 15
        rdma(mxs, rm1.at[p], sm1.at[p], sr1.at[p], partner).wait_recv()
        return carry

    lax.fori_loop(1, 2 * A, wait_max, 0)
    ring = jnp.max(rm1[...], axis=0)
    mxs2[...] = ring
    rm2[z] = ring

    def send_max2(k, carry):
        p = (z + k) & 7
        rdma(mxs2, rm2.at[z], sm2.at[p], sr2.at[z], (p, y, c, x)).start()
        return carry

    lax.fori_loop(1, A, send_max2, 0)
    raw_part(0)
    for j in range(7):
        rdma(offv, roff.at[j], so.at[0], ro.at[j], partner).wait_recv()
        dither(j, roff[j])

    def wait_max2(k, carry):
        p = (z + k) & 7
        rdma(mxs2, rm2.at[p], sm2.at[p], sr2.at[p], partner).wait_recv()
        return carry

    lax.fori_loop(1, A, wait_max2, 0)
    best = jnp.broadcast_to(jnp.max(rm2[...], axis=0), (ROWS, 128))
    step = jnp.full((ROWS, 128), 2.0 ** (low_power - 6), jnp.float32)
    inverse = jnp.full((ROWS, 128), 2.0 ** (6 - low_power + 20), jnp.float32)
    for e in range(low_power, high_power):
        over = best >= 2.0**e
        step = jnp.where(over, jnp.float32(2.0 ** (e - 5)), step)
        inverse = jnp.where(over, jnp.float32(2.0 ** (25 - e)), inverse)

    def pick(value, block):
        index = jnp.full((ROWS, 128), block, jnp.int32)
        return jnp.take_along_axis(value, index, axis=1, mode="promise_in_bounds")

    for mz in range(H):
        for my in range(H):
            scl[mz, my] = pick(inverse, c * A * A + dest(z, c, False, mz) * A + dest(y, c, False, my))
    stp_s[...] = pick(step, c * A * A + z * A + y)

    def sum_send(mz, my):
        dev = (dest(z, c, False, mz), dest(y, c, False, my), c, x)
        return rdma(sums.at[mz, my], rc.at[mz, my], s1.at[mz, my], r1.at[mz, my], dev)

    for mz in range(H - 1, -1, -1):
        for j in range(7):
            rdma(rp.at[j, mz], rp.at[j, mz], sraw.at[0], rr.at[j, mz], partner).wait_recv()

        def one(i, carry):
            my = H - 1 - i
            zp, yp = dest(z, c, False, mz), dest(y, c, False, my)
            scale = scl[mz, my]
            for t in range(TILES):
                cols = pl.ds(t * 128, 128)

                def rounded(tile, j):
                    whole = jnp.floor(tile.astype(jnp.float32) * scale).astype(jnp.int32)
                    return (whole + noise[j, mz, my, :, cols]) >> 20

                both = rounded(gv[c, zp, yp, :, cols], 7)
                for j in range(7):
                    both += rounded(rp[j, mz, my, :, cols], j)
                sums[mz, my, :, cols] = both.astype(jnp.int16)
            if mz:
                sum_send(mz, my).start()
            else:

                @pl.when(my > 0)
                def _():
                    sum_send(mz, my).start()

            return carry

        lax.fori_loop(0, H, one, 0)

    def gather(i, total):
        mz, my = i >> 2, i & 3
        sum_send(mz, my).wait_recv()
        return total + rc[mz, my].astype(jnp.int32)

    total = lax.fori_loop(1, H * H, gather, sums[0, 0].astype(jnp.int32)).astype(jnp.float32)
    own = stp_s[...]
    share = own * (1.0 / (2 * A * A))
    for t in range(TILES):
        rx[x, :, t * 128 : (t + 1) * 128] = total[:, t * 128 : (t + 1) * 128] * share
    rx[x, :, COLS:] = own

    def send_x(k, carry):
        xp = (x + k) & 3
        rdma(rx.at[x], rx.at[x], sx.at[xp], rxs.at[x], (z, y, c, xp)).start()
        return carry

    lax.fori_loop(1, X, send_x, 0)

    for i in range(7):
        rdma(offv, roff.at[i], so.at[i], ro.at[i], partner).wait_send()
        rdma(rp.at[i], rp.at[i], sraw.at[i], rr.at[i, 0], partner).wait_send()

    def drain15(i, carry):
        sum_send(i >> 2, i & 3).wait_send()
        return carry

    lax.fori_loop(1, H * H, drain15, 0)

    def drain16(k, carry):
        p = (me16 + k) & 15
        rdma(mxs, rm1.at[me16], sm1.at[p], sr1.at[me16], partner).wait_send()
        return carry

    lax.fori_loop(1, 2 * A, drain16, 0)

    def drain8(k, carry):
        rdma(mxs2, rm2.at[z], sm2.at[(z + k) & 7], sr2.at[z], partner).wait_send()
        return carry

    lax.fori_loop(1, A, drain8, 0)

    def wait_x(k, carry):
        xp = (x + k) & 3
        rdma(rx.at[xp], rx.at[xp], sx.at[xp], rxs.at[xp], partner).wait_recv()
        return carry

    lax.fori_loop(1, X, wait_x, 0)

    def drain4(k, carry):
        xp = (x + k) & 3
        rdma(rx.at[x], rx.at[x], sx.at[xp], rxs.at[x], partner).wait_send()
        return carry

    lax.fori_loop(1, X, drain4, 0)


def finish(rx, se_ref, mw_ref, mean_o, new_o, step_o):
    x = lax.axis_index("expert")
    value = rx[X - 1]
    for s in range(X - 1):
        value = jnp.where(se_ref[s] == x, rx[s], value)
    mean = value[:, :COLS]
    mean_o[...] = mean
    new_o[...] = mw_ref[...] - learn_rate * mean
    step_o[...] = value[0:1, COLS : COLS + 1]


def body(expert_grads, round_offsets, slot_expert, master_weight):
    f32, bf16, i32 = jnp.float32, jnp.bfloat16, jnp.int32
    dma = pltpu.SemaphoreType.DMA
    vmem = pl.BlockSpec(memory_space=pltpu.VMEM)
    hbm = pl.BlockSpec(memory_space=pl.ANY)
    gathered = pl.pallas_call(
        kernel,
        name="average",
        out_shape=pltpu.VMEM((X, ROWS, COLS + 128), f32),
        in_specs=[hbm, hbm],
        out_specs=vmem,
        scratch_shapes=[
            pltpu.VMEM((2, A, A, ROWS, COLS), bf16),
            pltpu.VMEM((7, H, H, ROWS, COLS), bf16),
            pltpu.VMEM((A, 128), i32),
            pltpu.VMEM((7, A, 128), i32),
            pltpu.VMEM((8, 128, 128), i32),
            pltpu.VMEM((8, H, H, ROWS, COLS), i32),
            pltpu.VMEM((2 * A * A * ROWS, 128), f32),
            pltpu.VMEM((1, 128), f32),
            pltpu.VMEM((2 * A, 1, 128), f32),
            pltpu.VMEM((1, 128), f32),
            pltpu.VMEM((A, 1, 128), f32),
            pltpu.VMEM((ROWS, 128), f32),
            pltpu.VMEM((H, H, ROWS, 128), f32),
            pltpu.VMEM((H, H, ROWS, COLS), jnp.int16),
            pltpu.VMEM((H, H, ROWS, COLS), jnp.int16),
            dma((CHUNKS, 2)),
            dma((1,)),
            dma((7,)),
            dma((7,)),
            dma((7,)),
            dma((7, H)),
            dma((2 * A,)),
            dma((2 * A,)),
            dma((A,)),
            dma((A,)),
            dma((H, H)),
            dma((H, H)),
            dma((X,)),
            dma((X,)),
        ],
        compiler_params=pltpu.CompilerParams(collective_id=0, has_side_effects=True),
    )(expert_grads.reshape(A, A, 2, ROWS, COLS), round_offsets.reshape(A, 128))
    mean, new, step = pl.pallas_call(
        finish,
        name="finish",
        out_shape=(
            jax.ShapeDtypeStruct((ROWS, COLS), f32),
            jax.ShapeDtypeStruct((ROWS, COLS), f32),
            jax.ShapeDtypeStruct((1, 1), f32),
        ),
        in_specs=[vmem, pl.BlockSpec(memory_space=pltpu.SMEM), vmem],
        out_specs=(vmem, vmem, vmem),
        compiler_params=pltpu.CompilerParams(vmem_limit_bytes=1024 * 1024),
    )(gathered, slot_expert, master_weight.reshape(ROWS, COLS))
    return mean[None], new[None], step


def solution(mesh):
    finer = Mesh(
        mesh.devices.reshape(A, A, 2, mesh.shape["expert"]), ("dp_0", "dp_1", "dp_2", "expert")
    )
    return jax.shard_map(
        body,
        mesh=finer,
        in_specs=(P(DP, "expert", None, None), P(DP, "expert", None), P(), P("expert", DP, None)),
        out_specs=(P("expert", DP, None), P("expert", DP, None), P("expert", DP)),
        check_vma=False,
    )
```

time: 42.8 us -> 41.5 us (0.970)
  the two profiles are of different devices: /device:TPU:64 before, /device:TPU:72 now
where the time goes in v3:
time: 41.5 us; the launch traced here: 41.3 us
  Pallas kernels  40.6 us (98%)
  between operations  0.67 us (2%)
    pallas_call x1, Pallas kernels, body(): pl.pallas_call(kernel, name='average', out_shape=pltpu.VMEM((X, ROWS, COL...  39.5 us
    pallas_call x1, Pallas kernels, body(): pl.pallas_call(finish, name='finish', out_shape=(jax.ShapeDtypeStruct((RO...  1.18 us

profile of v3, /device:TPU:72, one launch (start us, length us, event | category | flops | bytes accessed | tf_op | source)
XLA Modules:
  0.0 41.3 jit_solution(11677457479128527832)
XLA Ops:
  0.6 0.0 copy-start
  0.6 0.0 copy-start.1
  0.7 39.5 %average.1.rx = f32[4,8,1024]{2,1,0:T(8,128)S(1)} custom-call(bf16[8,8,2,8,896]{4,3,2,1,0:T(8,128)(2,1)} %bitcast.6, s32[8,128]{1,0:T(8,128)} %bitcast.7), custom_call_target="tpu_custom_call" | custom-call | tf_op jit(solution)/shard_map/average/pallas_call | solution.py:325
  40.1 0.0 copy-done
  40.1 0.0 copy-done.1
  40.1 1.2 %finish.1 = (f32[8,896]{1,0:T(8,128)}, f32[8,896]{1,0:T(8,128)}, f32[1,1]{1,0:T(1,128)}) custom-call(f32[4,8,1024]{2,1,0:T(8,128)S(1)} %average.1.rx, s32[4]{0:T(128)S(1)} %copy-done.1, f32[8,896]{1,0:T(8,128)S(1)} %bitcast.5), custom_call_target="tpu_custom_call" | custom-call | tf_op jit(solution)/shard_map/finish/pallas_call | solution.py:364
Async XLA Ops:
  0.6 39.5 %copy-start = (f32[1,8,896]{2,1,0:T(8,128)S(1)}, f32[1,8,896]{2,1,0:T(8,128)}, u32[]{:S(2)}) copy-start(f32[1,8,896]{2,1,0:T(8,128)} %param.7) | copy-start | bytes 86020
  0.6 39.5 %copy-start.1 = (s32[4]{0:T(128)S(1)}, s32[4]{0:T(128)}, u32[]{:S(2)}) copy-start(s32[4]{0:T(128)} %se_ref.1) | copy-start | bytes 52

commit v4 on v3

v4 whole, which is shorter than its diff:
```python
import jax
import jax.numpy as jnp
from jax import lax
from jax.experimental import pallas as pl
from jax.experimental.pallas import tpu as pltpu
from jax.sharding import Mesh
from jax.sharding import PartitionSpec as P

DP = ("dp_0", "dp_1", "dp_2")
MESH = pl.DeviceIdType.MESH
A = 8
X = 4
H = A // 2
ROWS = 8
COLS = 896
TILES = COLS // 128
CHUNKS = 4
low_power = -30
high_power = 30
learn_rate = 0.05
HASH_MUL = 747796405
HASH_ADD = 1013904223
HASH_MIX = 1103515245


def plan():
    tasks = []
    for mz in range(H):
        for my in range(H):
            along_y = mz + my > 1 or my > mz
            along_z = mz + my > 1 or mz > my
            for fz in (mz,) if along_z else (mz, -1 - mz):
                for fy in (my,) if along_y else (my, -1 - my):
                    tasks.append((fz, fy, along_y, along_z))

    def hops(task):
        return sum(f if f >= 0 else -f for f in task[:2])

    return sorted(tasks, key=lambda task: (-hops(task), task))


TASKS = plan()
N = len(TASKS)
OF = [
    list(range(N)),
    [i for i in range(N) if TASKS[i][2]],
    [i for i in range(N) if TASKS[i][3]],
    [i for i in range(N) if TASKS[i][2] and TASKS[i][3]],
]
WAVES = [range(N * w // 4, N * (w + 1) // 4) for w in range(4)]
SIZES = [len(OF[q]) for q in (0, 1, 1, 2, 2, 3, 3, 0)]
BASE = [sum(SIZES[:j]) for j in range(8)]
FIRST = (0.5, 1.0, 0.4, 1.0)
SENDS = [
    [(q, i) for i in range(N) for q in (3, 1, 2, 0) if i in OF[q] and (OF[q].index(i) < FIRST[q] * len(OF[q])) == early]
    for early in (True, False)
]


def kernel(
    g_hbm, off_hbm, rx,
    gv, rp0, rp1, rp2, rp3, offv, roff, toff, codes, noise, pm, mxs, rm1, mxs2, rm2, stp_s, scl, sums, rc,
    ld, lo, so, ro, sraw, rr, sm1, sr1, sm2, sr2, s1, r1, sx, rxs,
):
    z, y, c, x = (lax.axis_index(n) for n in ("dp_0", "dp_1", "dp_2", "expert"))

    def rdma(src, dst, send, recv, dev):
        return pltpu.make_async_remote_copy(
            src_ref=src, dst_ref=dst, send_sem=send, recv_sem=recv, device_id=dev, device_id_type=MESH
        )

    partner = (z, y, 1 - c, x)
    per = A // CHUNKS

    def way(position, core):
        return 2 * ((position + core) & 1) - 1

    def load(q, h):
        rows = pl.ds(q * per, per)
        return pltpu.make_async_copy(g_hbm.at[rows, :, h], gv.at[h, rows], ld.at[q, h])

    load_off = pltpu.make_async_copy(off_hbm, offv, lo.at[0])
    load_off.start()
    for q in range(CHUNKS):
        for h in range(2):
            load(q, h).start()

    barrier = pltpu.get_barrier_semaphore()
    me16 = y * 2 + c
    mz16 = z * 2 + c

    def greet(dev):
        pl.semaphore_signal(barrier, inc=1, device_id=dev, device_id_type=MESH)

    def greet16(k, carry):
        p = (me16 + k) & 15
        greet((z, p >> 1, p & 1, x))
        return carry

    def greet14(k, carry):
        p = (mz16 + k) & 15

        @pl.when((p >> 1) != z)
        def _():
            greet((p >> 1, y, p & 1, x))

        return carry

    def greet4(k, carry):
        greet((z, y, c, (x + k) & 3))
        return carry

    def near(position, core):
        return (position - way(position, core)) & 7

    lax.fori_loop(1, 2 * A, greet16, 0)
    lax.fori_loop(1, 2 * A, greet14, 0)
    lax.fori_loop(1, X, greet4, 0)
    greet((near(z, c), near(y, c), c, x))
    greet((near(z, c), near(y, c), 1 - c, x))
    greet((near(z, 1 - c), near(y, 1 - c), 1 - c, x))

    for q in range(CHUNKS):
        for h in range(2):
            load(q, h).wait()

            def block_max(i, carry):
                v = jnp.abs(gv[h, i >> 3, i & 7].astype(jnp.float32))
                m = v[:, :128]
                for t in range(1, TILES):
                    m = jnp.maximum(m, v[:, t * 128 : (t + 1) * 128])
                pm[pl.ds((h * A * A + i) * ROWS, ROWS), :] = m
                return carry

            lax.fori_loop(q * per * A, (q + 1) * per * A, block_max, 0, unroll=4)
    top = pm[pl.ds(0, 128, stride=ROWS), :]
    for r in range(1, ROWS):
        top = jnp.maximum(top, pm[pl.ds(r, 128, stride=ROWS), :])
    mine = jnp.max(top.T, axis=0, keepdims=True)
    mxs[...] = mine
    rm1[me16] = mine
    load_off.wait()

    pl.semaphore_wait(barrier, (2 * A - 1) + (2 * A - 2) + (X - 1) + 3)

    def send_max(k, carry):
        p = (y + k) & 7

        @pl.when(k + 1 - c != 0)
        def _():
            rdma(mxs, rm1.at[me16], sm1.at[p], sr1.at[me16], (z, p, 1, x)).start()

        return carry

    lax.fori_loop(0, A, send_max, 0)

    def to_near(core, q):
        return (near(z, core) if q > 1 else z, y if q == 2 else near(y, core), core, x)

    def dest(position, core, f):
        return (position + way(position, core) * f) & 7

    def spot(i, core=c, q=0):
        fz, fy = TASKS[i][:2]
        return dest(z, core, -1 - fz if q > 1 else fz), dest(y, core, -1 - fy if q in (1, 3) else fy)

    def group(q, wave):
        inside = [n for n, i in enumerate(OF[q]) if i in WAVES[wave]]
        return pl.ds(inside[0], len(inside)) if inside else None

    sources = [(0, 0)] + [(q, k) for q in (1, 2, 3) for k in range(2)]
    buffers = (rp0, rp1, rp2, rp3)

    def buffer(j):
        q, k = sources[j]
        return buffers[q] if q == 0 else buffers[q].at[k]

    rdma(offv, roff.at[0], so.at[0], ro.at[0], partner).start()
    for core in range(2):
        for q in (1, 2, 3):
            slot = 2 * q - 1 + c
            rdma(offv, roff.at[slot], so.at[3 * core + q], ro.at[slot], to_near(core, q)).start()

    def raw_send(q, i):
        wave = [w for w in range(len(WAVES)) if i in WAVES[w]][0]
        if q == 0:
            zp, yp = spot(i, 1 - c)
            rdma(gv.at[1 - c, zp, yp], rp0.at[i], sraw.at[0], rr.at[0, wave], partner).start()
            return
        n = OF[q].index(i)
        for core in range(2):
            zp, yp = spot(i, core, q)
            rdma(
                gv.at[core, zp, yp], buffers[q].at[c, n], sraw.at[3 * core + q], rr.at[2 * q - 1 + c, wave],
                to_near(core, q),
            ).start()

    for q, i in SENDS[0]:
        raw_send(q, i)

    lane = lax.broadcasted_iota(jnp.int32, (ROWS, 128), 1)
    column = [(lane + t * 128) * HASH_MUL for t in range(TILES)]

    def dither(j, value):
        start = value * HASH_MUL + HASH_ADD
        toff[...] = jnp.concatenate([start] * 16, axis=0).T
        q = 0 if j == 7 else sources[j][0]
        for n, i in enumerate(OF[q]):
            zp, yp = spot(i)
            tile = toff[pl.ds((yp * 2 + c) * ROWS, ROWS), :]
            index = jnp.full((ROWS, 128), zp, jnp.int32)
            codes[n] = jnp.take_along_axis(tile, index, axis=1, mode="promise_in_bounds")

        def one(n, carry):
            code = codes[n]
            for t in range(TILES):
                v = code + column[t]
                v = v ^ (v >> 13)
                v = v * HASH_MIX
                v = v ^ (v >> 16)
                noise[BASE[j] + n, :, pl.ds(t * 128, 128)] = v & 0xFF000
            return carry

        lax.fori_loop(0, len(OF[q]), one, 0)

    dither(7, offv[...])

    @pl.when(c == 1)
    def _():
        def wait_max(k, carry):
            p = (me16 + k) & 15
            rdma(mxs, rm1.at[p], sm1.at[0], sr1.at[p], partner).wait_recv()
            return carry

        lax.fori_loop(1, 2 * A, wait_max, 0)
        ring = jnp.max(rm1[...], axis=0)
        mxs2[...] = ring
        rm2[z] = ring

        def send_max2(k, carry):
            p = (mz16 + k) & 15
            rdma(mxs2, rm2.at[z], sm2.at[p], sr2.at[z], (p >> 1, y, p & 1, x)).start()
            return carry

        lax.fori_loop(1, 2 * A, send_max2, 0)

    for q, i in SENDS[1]:
        raw_send(q, i)
    for j in range(7):
        rdma(offv, roff.at[j], so.at[0], ro.at[j], partner).wait_recv()
        dither(j, roff[j])

    def wait_max2(k, carry):
        p = (z + k) & 7

        @pl.when(k + 1 - c != 0)
        def _():
            rdma(mxs2, rm2.at[p], sm2.at[p], sr2.at[p], partner).wait_recv()

        return carry

    lax.fori_loop(0, A, wait_max2, 0)
    best = jnp.broadcast_to(jnp.max(rm2[...], axis=0), (ROWS, 128))
    step = jnp.full((ROWS, 128), 2.0 ** (low_power - 6), jnp.float32)
    inverse = jnp.full((ROWS, 128), 2.0 ** (6 - low_power + 20), jnp.float32)
    for e in range(low_power, high_power):
        over = best >= 2.0**e
        step = jnp.where(over, jnp.float32(2.0 ** (e - 5)), step)
        inverse = jnp.where(over, jnp.float32(2.0 ** (25 - e)), inverse)

    def pick(value, block):
        index = jnp.full((ROWS, 128), block, jnp.int32)
        return jnp.take_along_axis(value, index, axis=1, mode="promise_in_bounds")

    for i in range(N):
        zp, yp = spot(i)
        scl[i] = pick(inverse, c * A * A + zp * A + yp)
    stp_s[...] = pick(step, c * A * A + z * A + y)

    def sum_send(i):
        zp, yp = spot(i)
        return rdma(sums.at[i], rc.at[i], s1.at[i], r1.at[i], (zp, yp, c, x))

    for wave in range(len(WAVES)):
        for j in range(7):
            rows = group(sources[j][0], wave)
            if rows is not None:
                rdma(buffer(j).at[rows], buffer(j).at[rows], sraw.at[0], rr.at[j, wave], partner).wait_recv()
        for i in WAVES[wave]:
            zp, yp = spot(i)
            scale = scl[i]
            parts = [(gv.at[c, zp, yp], BASE[7] + i)]
            for j in range(7):
                q = sources[j][0]
                if i in OF[q]:
                    n = OF[q].index(i)
                    parts.append((buffer(j).at[n], BASE[j] + n))

            def tile(t, carry):
                cols = pl.ds(pl.multiple_of(t * 128, 128), 128)
                both = None
                for rows, n in parts:
                    whole = jnp.floor(rows[:, cols].astype(jnp.float32) * scale).astype(jnp.int32)
                    part = (whole + noise[n, :, cols]) >> 20
                    both = part if both is None else both + part
                sums[i, :, cols] = both.astype(jnp.int16)
                return carry

            lax.fori_loop(0, TILES, tile, 0, unroll=True)
            if i < N - 1:
                sum_send(i).start()

    total = sums[N - 1].astype(jnp.int32)
    for i in range(N - 1):
        sum_send(i).wait_recv()
        total += rc[i].astype(jnp.int32)
    total = total.astype(jnp.float32)
    own = stp_s[...]
    share = own * (1.0 / (2 * A * A))
    for t in range(TILES):
        rx[x, :, t * 128 : (t + 1) * 128] = total[:, t * 128 : (t + 1) * 128] * share
    rx[x, :, COLS:] = own

    def send_x(k, carry):
        xp = (x + k) & 3
        rdma(rx.at[x], rx.at[x], sx.at[xp], rxs.at[x], (z, y, c, xp)).start()
        return carry

    lax.fori_loop(1, X, send_x, 0)

    for i in range(7):
        rdma(offv, roff.at[i], so.at[i], ro.at[i], partner).wait_send()
    for i in range(7):
        rows = buffers[(i + 2) % 3 + 1 if i else 0]
        rows = rows if i == 0 else rows.at[0]
        rdma(rows, rows, sraw.at[i], rr.at[0, 0], partner).wait_send()
    for i in range(N - 1):
        sum_send(i).wait_send()

    def drain8(k, carry):
        @pl.when(k + 1 - c != 0)
        def _():
            rdma(mxs, rm1.at[me16], sm1.at[(y + k) & 7], sr1.at[me16], partner).wait_send()

        return carry

    lax.fori_loop(0, A, drain8, 0)

    @pl.when(c == 1)
    def _():
        def drain16(k, carry):
            rdma(mxs2, rm2.at[z], sm2.at[(mz16 + k) & 15], sr2.at[z], partner).wait_send()
            return carry

        lax.fori_loop(1, 2 * A, drain16, 0)

    def wait_x(k, carry):
        xp = (x + k) & 3
        rdma(rx.at[xp], rx.at[xp], sx.at[xp], rxs.at[xp], partner).wait_recv()
        return carry

    lax.fori_loop(1, X, wait_x, 0)

    def drain4(k, carry):
        xp = (x + k) & 3
        rdma(rx.at[x], rx.at[x], sx.at[xp], rxs.at[x], partner).wait_send()
        return carry

    lax.fori_loop(1, X, drain4, 0)


def finish(rx, se_ref, mw_ref, mean_o, new_o, step_o):
    x = lax.axis_index("expert")
    value = rx[X - 1]
    for s in range(X - 1):
        value = jnp.where(se_ref[s] == x, rx[s], value)
    mean = value[:, :COLS]
    mean_o[...] = mean
    new_o[...] = mw_ref[...] - learn_rate * mean
    step_o[...] = value[0:1, COLS : COLS + 1]


def body(expert_grads, round_offsets, slot_expert, master_weight):
    f32, bf16, i32 = jnp.float32, jnp.bfloat16, jnp.int32
    dma = pltpu.SemaphoreType.DMA
    vmem = pl.BlockSpec(memory_space=pltpu.VMEM)
    hbm = pl.BlockSpec(memory_space=pl.ANY)
    gathered = pl.pallas_call(
        kernel,
        name="average",
        out_shape=pltpu.VMEM((X, ROWS, COLS + 128), f32),
        in_specs=[hbm, hbm],
        out_specs=vmem,
        scratch_shapes=[
            pltpu.VMEM((2, A, A, ROWS, COLS), bf16),
            pltpu.VMEM((N, ROWS, COLS), bf16),
            pltpu.VMEM((2, len(OF[1]), ROWS, COLS), bf16),
            pltpu.VMEM((2, len(OF[2]), ROWS, COLS), bf16),
            pltpu.VMEM((2, len(OF[3]), ROWS, COLS), bf16),
            pltpu.VMEM((A, 128), i32),
            pltpu.VMEM((7, A, 128), i32),
            pltpu.VMEM((128, 128), i32),
            pltpu.VMEM((N, ROWS, 128), i32),
            pltpu.VMEM((sum(SIZES), ROWS, COLS), i32),
            pltpu.VMEM((2 * A * A * ROWS, 128), f32),
            pltpu.VMEM((1, 128), f32),
            pltpu.VMEM((2 * A, 1, 128), f32),
            pltpu.VMEM((1, 128), f32),
            pltpu.VMEM((A, 1, 128), f32),
            pltpu.VMEM((ROWS, 128), f32),
            pltpu.VMEM((N, ROWS, 128), f32),
            pltpu.VMEM((N, ROWS, COLS), jnp.int16),
            pltpu.VMEM((N, ROWS, COLS), jnp.int16),
            dma((CHUNKS, 2)),
            dma((1,)),
            dma((7,)),
            dma((7,)),
            dma((7,)),
            dma((7, len(WAVES))),
            dma((A,)),
            dma((2 * A,)),
            dma((2 * A,)),
            dma((A,)),
            dma((N,)),
            dma((N,)),
            dma((X,)),
            dma((X,)),
        ],
        compiler_params=pltpu.CompilerParams(collective_id=0, has_side_effects=True),
    )(expert_grads.reshape(A, A, 2, ROWS, COLS), round_offsets.reshape(A, 128))
    mean, new, step = pl.pallas_call(
        finish,
        name="finish",
        out_shape=(
            jax.ShapeDtypeStruct((ROWS, COLS), f32),
            jax.ShapeDtypeStruct((ROWS, COLS), f32),
            jax.ShapeDtypeStruct((1, 1), f32),
        ),
        in_specs=[vmem, pl.BlockSpec(memory_space=pltpu.SMEM), vmem],
        out_specs=(vmem, vmem, vmem),
        compiler_params=pltpu.CompilerParams(vmem_limit_bytes=1024 * 1024),
    )(gathered, slot_expert, master_weight.reshape(ROWS, COLS))
    return mean[None], new[None], step


def solution(mesh):
    finer = Mesh(
        mesh.devices.reshape(A, A, 2, mesh.shape["expert"]), ("dp_0", "dp_1", "dp_2", "expert")
    )
    return jax.shard_map(
        body,
        mesh=finer,
        in_specs=(P(DP, "expert", None, None), P(DP, "expert", None), P(), P("expert", DP, None)),
        out_specs=(P("expert", DP, None), P("expert", DP, None), P("expert", DP)),
        check_vma=False,
    )
```

time: 41.5 us -> 38.6 us (0.930)
  the two profiles are of different devices: /device:TPU:72 before, /device:TPU:1 now
where the time goes in v4:
time: 38.6 us; the launch traced here: 38.4 us
  Pallas kernels  37.7 us (98%)
  between operations  0.67 us (2%)
    pallas_call x1, Pallas kernels, body(): pl.pallas_call(kernel, name='average', out_shape=pltpu.VMEM((X, ROWS, COL...  36.6 us
    pallas_call x1, Pallas kernels, body(): pl.pallas_call(finish, name='finish', out_shape=(jax.ShapeDtypeStruct((RO...  1.18 us

profile of v4, /device:TPU:1, one launch (start us, length us, event | category | flops | bytes accessed | tf_op | source)
XLA Modules:
  0.0 38.4 jit_solution(15230482909467400727)
XLA Ops:
  0.6 0.0 copy-start
  0.6 0.0 copy-start.1
  0.7 36.6 %average.1.rx = f32[4,8,1024]{2,1,0:T(8,128)S(1)} custom-call(bf16[8,8,2,8,896]{4,3,2,1,0:T(8,128)(2,1)} %bitcast.6, s32[8,128]{1,0:T(8,128)} %bitcast.7), custom_call_target="tpu_custom_call" | custom-call | tf_op jit(solution)/shard_map/average/pallas_call | solution.py:388
  37.2 0.0 copy-done
  37.2 0.0 copy-done.1
  37.2 1.2 %finish.1 = (f32[8,896]{1,0:T(8,128)}, f32[8,896]{1,0:T(8,128)}, f32[1,1]{1,0:T(1,128)}) custom-call(f32[4,8,1024]{2,1,0:T(8,128)S(1)} %average.1.rx, s32[4]{0:T(128)S(1)} %copy-done.1, f32[8,896]{1,0:T(8,128)S(1)} %bitcast.5), custom_call_target="tpu_custom_call" | custom-call | tf_op jit(solution)/shard_map/finish/pallas_call | solution.py:431
Async XLA Ops:
  0.6 36.6 %copy-start = (f32[1,8,896]{2,1,0:T(8,128)S(1)}, f32[1,8,896]{2,1,0:T(8,128)}, u32[]{:S(2)}) copy-start(f32[1,8,896]{2,1,0:T(8,128)} %param.7) | copy-start | bytes 86020
  0.6 36.6 %copy-start.1 = (s32[4]{0:T(128)S(1)}, s32[4]{0:T(128)}, u32[]{:S(2)}) copy-start(s32[4]{0:T(128)} %se_ref.1) | copy-start | bytes 52

commit v5 on v4

--- a/solution.py
+++ b/solution.py
@@ -59,7 +59,7 @@
 
 def kernel(
     g_hbm, off_hbm, rx,
-    gv, rp0, rp1, rp2, rp3, offv, roff, toff, codes, noise, pm, mxs, rm1, mxs2, rm2, stp_s, scl, sums, rc,
+    gv, rp, offv, roff, toff, codes, noise, pm, mxs, rm1, mxs2, rm2, stp_s, scl, sums, rc,
     ld, lo, so, ro, sraw, rr, sm1, sr1, sm2, sr2, s1, r1, sx, rxs,
 ):
     z, y, c, x = (lax.axis_index(n) for n in ("dp_0", "dp_1", "dp_2", "expert"))
@@ -148,7 +148,7 @@
 
         @pl.when(k + 1 - c != 0)
         def _():
-            rdma(mxs, rm1.at[me16], sm1.at[p], sr1.at[me16], (z, p, 1, x)).start()
+            rdma(mxs, rm1.at[me16], sm1.at[0], sr1.at[0], (z, p, 1, x)).start()
 
         return carry
 
@@ -164,16 +164,7 @@
         fz, fy = TASKS[i][:2]
         return dest(z, core, -1 - fz if q > 1 else fz), dest(y, core, -1 - fy if q in (1, 3) else fy)
 
-    def group(q, wave):
-        inside = [n for n, i in enumerate(OF[q]) if i in WAVES[wave]]
-        return pl.ds(inside[0], len(inside)) if inside else None
-
     sources = [(0, 0)] + [(q, k) for q in (1, 2, 3) for k in range(2)]
-    buffers = (rp0, rp1, rp2, rp3)
-
-    def buffer(j):
-        q, k = sources[j]
-        return buffers[q] if q == 0 else buffers[q].at[k]
 
     rdma(offv, roff.at[0], so.at[0], ro.at[0], partner).start()
     for core in range(2):
@@ -185,14 +176,13 @@
         wave = [w for w in range(len(WAVES)) if i in WAVES[w]][0]
         if q == 0:
             zp, yp = spot(i, 1 - c)
-            rdma(gv.at[1 - c, zp, yp], rp0.at[i], sraw.at[0], rr.at[0, wave], partner).start()
+            rdma(gv.at[1 - c, zp, yp], rp.at[i], sraw.at[0], rr.at[wave], partner).start()
             return
         n = OF[q].index(i)
         for core in range(2):
             zp, yp = spot(i, core, q)
             rdma(
-                gv.at[core, zp, yp], buffers[q].at[c, n], sraw.at[3 * core + q], rr.at[2 * q - 1 + c, wave],
-                to_near(core, q),
+                gv.at[core, zp, yp], rp.at[BASE[2 * q - 1] + c * len(OF[q]) + n], sraw.at[0], rr.at[wave], to_near(core, q)
             ).start()
 
     for q, i in SENDS[0]:
@@ -227,19 +217,15 @@
 
     @pl.when(c == 1)
     def _():
-        def wait_max(k, carry):
-            p = (me16 + k) & 15
-            rdma(mxs, rm1.at[p], sm1.at[0], sr1.at[p], partner).wait_recv()
-            return carry
-
-        lax.fori_loop(1, 2 * A, wait_max, 0)
+        others = rm1.at[pl.ds(0, 2 * A - 1)]
+        rdma(others, others, sm1.at[0], sr1.at[0], partner).wait_recv()
         ring = jnp.max(rm1[...], axis=0)
         mxs2[...] = ring
         rm2[z] = ring
 
         def send_max2(k, carry):
             p = (mz16 + k) & 15
-            rdma(mxs2, rm2.at[z], sm2.at[p], sr2.at[z], (p >> 1, y, p & 1, x)).start()
+            rdma(mxs2, rm2.at[z], sm2.at[0], sr2.at[0], (p >> 1, y, p & 1, x)).start()
             return carry
 
         lax.fori_loop(1, 2 * A, send_max2, 0)
@@ -250,16 +236,13 @@
         rdma(offv, roff.at[j], so.at[0], ro.at[j], partner).wait_recv()
         dither(j, roff[j])
 
-    def wait_max2(k, carry):
-        p = (z + k) & 7
-
-        @pl.when(k + 1 - c != 0)
+    for core in range(2):
+
+        @pl.when(c == core)
         def _():
-            rdma(mxs2, rm2.at[p], sm2.at[p], sr2.at[p], partner).wait_recv()
-
-        return carry
-
-    lax.fori_loop(0, A, wait_max2, 0)
+            others = rm2.at[pl.ds(0, A - core)]
+            rdma(others, others, sm2.at[0], sr2.at[0], partner).wait_recv()
+
     best = jnp.broadcast_to(jnp.max(rm2[...], axis=0), (ROWS, 128))
     step = jnp.full((ROWS, 128), 2.0 ** (low_power - 6), jnp.float32)
     inverse = jnp.full((ROWS, 128), 2.0 ** (6 - low_power + 20), jnp.float32)
@@ -279,13 +262,11 @@
 
     def sum_send(i):
         zp, yp = spot(i)
-        return rdma(sums.at[i], rc.at[i], s1.at[i], r1.at[i], (zp, yp, c, x))
+        return rdma(sums.at[i], rc.at[i], s1.at[0], r1.at[0 if i < N // 2 else 1], (zp, yp, c, x))
 
     for wave in range(len(WAVES)):
-        for j in range(7):
-            rows = group(sources[j][0], wave)
-            if rows is not None:
-                rdma(buffer(j).at[rows], buffer(j).at[rows], sraw.at[0], rr.at[j, wave], partner).wait_recv()
+        arrived = rp.at[pl.ds(0, sum(i in WAVES[wave] for q, _ in sources for i in OF[q]))]
+        rdma(arrived, arrived, sraw.at[0], rr.at[wave], partner).wait_recv()
         for i in WAVES[wave]:
             zp, yp = spot(i)
             scale = scl[i]
@@ -294,7 +275,7 @@
                 q = sources[j][0]
                 if i in OF[q]:
                     n = OF[q].index(i)
-                    parts.append((buffer(j).at[n], BASE[j] + n))
+                    parts.append((rp.at[BASE[j] + n], BASE[j] + n))
 
             def tile(t, carry):
                 cols = pl.ds(pl.multiple_of(t * 128, 128), 128)
@@ -311,9 +292,11 @@
                 sum_send(i).start()
 
     total = sums[N - 1].astype(jnp.int32)
-    for i in range(N - 1):
-        sum_send(i).wait_recv()
-        total += rc[i].astype(jnp.int32)
+    for part, rows in enumerate((range(N // 2), range(N // 2, N - 1))):
+        half = rc.at[pl.ds(rows[0], len(rows))]
+        rdma(half, half, s1.at[0], r1.at[part], partner).wait_recv()
+        for i in rows:
+            total += rc[i].astype(jnp.int32)
     total = total.astype(jnp.float32)
     own = stp_s[...]
     share = own * (1.0 / (2 * A * A))
@@ -323,57 +306,37 @@
 
     def send_x(k, carry):
         xp = (x + k) & 3
-        rdma(rx.at[x], rx.at[x], sx.at[xp], rxs.at[x], (z, y, c, xp)).start()
+        rdma(rx.at[x], rx.at[x], sx.at[0], rxs.at[0], (z, y, c, xp)).start()
         return carry
 
-    lax.fori_loop(1, X, send_x, 0)
+    for k in (2, 1, 3):
+        send_x(k, 0)
 
     for i in range(7):
         rdma(offv, roff.at[i], so.at[i], ro.at[i], partner).wait_send()
-    for i in range(7):
-        rows = buffers[(i + 2) % 3 + 1 if i else 0]
-        rows = rows if i == 0 else rows.at[0]
-        rdma(rows, rows, sraw.at[i], rr.at[0, 0], partner).wait_send()
-    for i in range(N - 1):
-        sum_send(i).wait_send()
-
-    def drain8(k, carry):
-        @pl.when(k + 1 - c != 0)
+    rdma(rp, rp, sraw.at[0], rr.at[0], partner).wait_send()
+    rdma(rc.at[pl.ds(0, N - 1)], rc.at[pl.ds(0, N - 1)], s1.at[0], r1.at[0], partner).wait_send()
+
+    for core in range(2):
+
+        @pl.when(c == core)
         def _():
-            rdma(mxs, rm1.at[me16], sm1.at[(y + k) & 7], sr1.at[me16], partner).wait_send()
-
-        return carry
-
-    lax.fori_loop(0, A, drain8, 0)
-
-    @pl.when(c == 1)
-    def _():
-        def drain16(k, carry):
-            rdma(mxs2, rm2.at[z], sm2.at[(mz16 + k) & 15], sr2.at[z], partner).wait_send()
-            return carry
-
-        lax.fori_loop(1, 2 * A, drain16, 0)
-
-    def wait_x(k, carry):
-        xp = (x + k) & 3
-        rdma(rx.at[xp], rx.at[xp], sx.at[xp], rxs.at[xp], partner).wait_recv()
-        return carry
-
-    lax.fori_loop(1, X, wait_x, 0)
-
-    def drain4(k, carry):
-        xp = (x + k) & 3
-        rdma(rx.at[x], rx.at[x], sx.at[xp], rxs.at[x], partner).wait_send()
-        return carry
-
-    lax.fori_loop(1, X, drain4, 0)
+            others = rm2.at[pl.ds(0, A - core)]
+            rdma(others, others, sm1.at[0], sr2.at[0], partner).wait_send()
+            if core:
+                others = rm1.at[pl.ds(0, 2 * A - 1)]
+                rdma(others, others, sm2.at[0], sr1.at[0], partner).wait_send()
+
+    others = rx.at[pl.ds(0, X - 1)]
+    rdma(others, others, sx.at[0], rxs.at[0], partner).wait_recv()
+    rdma(others, others, sx.at[0], rxs.at[0], partner).wait_send()
 
 
 def finish(rx, se_ref, mw_ref, mean_o, new_o, step_o):
     x = lax.axis_index("expert")
     value = rx[X - 1]
     for s in range(X - 1):
-        value = jnp.where(se_ref[s] == x, rx[s], value)
+        value = jnp.where(se_ref[:, s : s + 1] == x, rx[s], value)
     mean = value[:, :COLS]
     mean_o[...] = mean
     new_o[...] = mw_ref[...] - learn_rate * mean
@@ -393,10 +356,7 @@
         out_specs=vmem,
         scratch_shapes=[
             pltpu.VMEM((2, A, A, ROWS, COLS), bf16),
-            pltpu.VMEM((N, ROWS, COLS), bf16),
-            pltpu.VMEM((2, len(OF[1]), ROWS, COLS), bf16),
-            pltpu.VMEM((2, len(OF[2]), ROWS, COLS), bf16),
-            pltpu.VMEM((2, len(OF[3]), ROWS, COLS), bf16),
+            pltpu.VMEM((BASE[7], ROWS, COLS), bf16),
             pltpu.VMEM((A, 128), i32),
             pltpu.VMEM((7, A, 128), i32),
             pltpu.VMEM((128, 128), i32),
@@ -415,16 +375,16 @@
             dma((1,)),
             dma((7,)),
             dma((7,)),
-            dma((7,)),
-            dma((7, len(WAVES))),
-            dma((A,)),
-            dma((2 * A,)),
-            dma((2 * A,)),
-            dma((A,)),
-            dma((N,)),
-            dma((N,)),
-            dma((X,)),
-            dma((X,)),
+            dma((1,)),
+            dma((len(WAVES),)),
+            dma((1,)),
+            dma((1,)),
+            dma((1,)),
+            dma((1,)),
+            dma((1,)),
+            dma((2,)),
+            dma((1,)),
+            dma((1,)),
         ],
         compiler_params=pltpu.CompilerParams(collective_id=0, has_side_effects=True),
     )(expert_grads.reshape(A, A, 2, ROWS, COLS), round_offsets.reshape(A, 128))
@@ -436,10 +396,10 @@
             jax.ShapeDtypeStruct((ROWS, COLS), f32),
             jax.ShapeDtypeStruct((1, 1), f32),
         ),
-        in_specs=[vmem, pl.BlockSpec(memory_space=pltpu.SMEM), vmem],
+        in_specs=[vmem, vmem, vmem],
         out_specs=(vmem, vmem, vmem),
         compiler_params=pltpu.CompilerParams(vmem_limit_bytes=1024 * 1024),
-    )(gathered, slot_expert, master_weight.reshape(ROWS, COLS))
+    )(gathered, slot_expert.reshape(1, X), master_weight.reshape(ROWS, COLS))
     return mean[None], new[None], step
 
 

time: 38.6 us -> 36.8 us (0.953)
  the two profiles are of different devices: /device:TPU:1 before, /device:TPU:8 now
where the time goes in v5:
time: 36.8 us; the launch traced here: 36.6 us
  Pallas kernels  35.9 us (98%)
  between operations  0.67 us (2%)
    pallas_call x1, Pallas kernels, body(): pl.pallas_call(kernel, name='average', out_shape=pltpu.VMEM((X, ROWS, COL...  35.2 us

profile of v5, /device:TPU:8, one launch (start us, length us, event | category | flops | bytes accessed | tf_op | source)
XLA Modules:
  0.0 36.6 jit_solution(15339334324858048961)
XLA Ops:
  0.6 0.0 copy-start
  0.6 0.0 copy-start.1
  0.7 35.2 %average.1.rx = f32[4,8,1024]{2,1,0:T(8,128)S(1)} custom-call(bf16[8,8,2,8,896]{4,3,2,1,0:T(8,128)(2,1)} %bitcast.8, s32[8,128]{1,0:T(8,128)} %bitcast.9), custom_call_target="tpu_custom_call" | custom-call | tf_op jit(solution)/shard_map/average/pallas_call | solution.py:351
  35.9 0.0 copy-done
  35.9 0.0 copy-done.1
  35.9 0.7 %finish.1 = (f32[8,896]{1,0:T(8,128)}, f32[8,896]{1,0:T(8,128)}, f32[1,1]{1,0:T(1,128)}) custom-call(f32[4,8,1024]{2,1,0:T(8,128)S(1)} %average.1.rx, s32[1,4]{1,0:T(1,128)S(1)} %bitcast.7, f32[8,896]{1,0:T(8,128)S(1)} %bitcast.6), custom_call_target="tpu_custom_call" | custom-call | tf_op jit(solution)/shard_map/finish/pallas_call | solution.py:391
Async XLA Ops:
  0.6 35.3 %copy-start = (f32[1,8,896]{2,1,0:T(8,128)S(1)}, f32[1,8,896]{2,1,0:T(8,128)}, u32[]{:S(2)}) copy-start(f32[1,8,896]{2,1,0:T(8,128)} %param.7) | copy-start | bytes 86020
  0.6 35.3 %copy-start.1 = (s32[4]{0:T(128)S(1)}, s32[4]{0:T(128)}, u32[]{:S(2)}) copy-start(s32[4]{0:T(128)} %param.6) | copy-start | bytes 52

commit v6 on v5

--- a/solution.py
+++ b/solution.py
@@ -113,8 +113,10 @@
     def near(position, core):
         return (position - way(position, core)) & 7
 
-    lax.fori_loop(1, 2 * A, greet16, 0)
-    lax.fori_loop(1, 2 * A, greet14, 0)
+    far = sorted(range(1, 2 * A), key=lambda k: -min(k, 2 * A - k))
+    for k in far:
+        greet14(k, 0)
+        greet16(k, 0)
     lax.fori_loop(1, X, greet4, 0)
     greet((near(z, c), near(y, c), c, x))
     greet((near(z, c), near(y, c), 1 - c, x))

time: 36.8 us -> 36.6 us (level)
  no operation moved by 1% of the time
where the time goes in v6:
time: 36.6 us; the launch traced here: 36.4 us
  Pallas kernels  35.7 us (98%)
  between operations  0.67 us (2%)
    pallas_call x1, Pallas kernels, body(): pl.pallas_call(kernel, name='average', out_shape=pltpu.VMEM((X, ROWS, COL...  35 us

profile of v6, /device:TPU:8, one launch (start us, length us, event | category | flops | bytes accessed | tf_op | source)
XLA Modules:
  0.0 36.4 jit_solution(16894536614876443135)
XLA Ops:
  0.6 0.0 copy-start
  0.6 0.0 copy-start.1
  0.7 35.0 %average.1.rx = f32[4,8,1024]{2,1,0:T(8,128)S(1)} custom-call(bf16[8,8,2,8,896]{4,3,2,1,0:T(8,128)(2,1)} %bitcast.8, s32[8,128]{1,0:T(8,128)} %bitcast.9), custom_call_target="tpu_custom_call" | custom-call | tf_op jit(solution)/shard_map/average/pallas_call | solution.py:353
  35.7 0.0 copy-done
  35.7 0.0 copy-done.1
  35.7 0.7 %finish.1 = (f32[8,896]{1,0:T(8,128)}, f32[8,896]{1,0:T(8,128)}, f32[1,1]{1,0:T(1,128)}) custom-call(f32[4,8,1024]{2,1,0:T(8,128)S(1)} %average.1.rx, s32[1,4]{1,0:T(1,128)S(1)} %bitcast.7, f32[8,896]{1,0:T(8,128)S(1)} %bitcast.6), custom_call_target="tpu_custom_call" | custom-call | tf_op jit(solution)/shard_map/finish/pallas_call | solution.py:393
Async XLA Ops:
  0.6 35.1 %copy-start = (f32[1,8,896]{2,1,0:T(8,128)S(1)}, f32[1,8,896]{2,1,0:T(8,128)}, u32[]{:S(2)}) copy-start(f32[1,8,896]{2,1,0:T(8,128)} %param.7) | copy-start | bytes 86020
  0.6 35.1 %copy-start.1 = (s32[4]{0:T(128)S(1)}, s32[4]{0:T(128)}, u32[]{:S(2)}) copy-start(s32[4]{0:T(128)} %param.6) | copy-start | bytes 52

commit v7 on v6

--- a/solution.py
+++ b/solution.py
@@ -58,7 +58,7 @@
 
 
 def kernel(
-    g_hbm, off_hbm, rx,
+    g_hbm, off_hbm, rx, rstep,
     gv, rp, offv, roff, toff, codes, noise, pm, mxs, rm1, mxs2, rm2, stp_s, scl, sums, rc,
     ld, lo, so, ro, sraw, rr, sm1, sr1, sm2, sr2, s1, r1, sx, rxs,
 ):
@@ -299,16 +299,13 @@
         rdma(half, half, s1.at[0], r1.at[part], partner).wait_recv()
         for i in rows:
             total += rc[i].astype(jnp.int32)
-    total = total.astype(jnp.float32)
-    own = stp_s[...]
-    share = own * (1.0 / (2 * A * A))
-    for t in range(TILES):
-        rx[x, :, t * 128 : (t + 1) * 128] = total[:, t * 128 : (t + 1) * 128] * share
-    rx[x, :, COLS:] = own
+    rx[x] = total.astype(jnp.int16)
+    rstep[x] = stp_s[...]
 
     def send_x(k, carry):
         xp = (x + k) & 3
         rdma(rx.at[x], rx.at[x], sx.at[0], rxs.at[0], (z, y, c, xp)).start()
+        rdma(rstep.at[x], rstep.at[x], sx.at[1], rxs.at[1], (z, y, c, xp)).start()
         return carry
 
     for k in (2, 1, 3):
@@ -329,20 +326,28 @@
                 others = rm1.at[pl.ds(0, 2 * A - 1)]
                 rdma(others, others, sm2.at[0], sr1.at[0], partner).wait_send()
 
-    others = rx.at[pl.ds(0, X - 1)]
-    rdma(others, others, sx.at[0], rxs.at[0], partner).wait_recv()
-    rdma(others, others, sx.at[0], rxs.at[0], partner).wait_send()
-
-
-def finish(rx, se_ref, mw_ref, mean_o, new_o, step_o):
+    for n, ref in enumerate((rx, rstep)):
+        others = ref.at[pl.ds(0, X - 1)]
+        rdma(others, others, sx.at[n], rxs.at[n], partner).wait_recv()
+        rdma(others, others, sx.at[n], rxs.at[n], partner).wait_send()
+
+
+def finish(rx, rstep, se_ref, mw_ref, mean_o, new_o, step_o):
     x = lax.axis_index("expert")
-    value = rx[X - 1]
+    total = rx[X - 1].astype(jnp.int32)
+    step = rstep[X - 1]
     for s in range(X - 1):
-        value = jnp.where(se_ref[:, s : s + 1] == x, rx[s], value)
-    mean = value[:, :COLS]
-    mean_o[...] = mean
-    new_o[...] = mw_ref[...] - learn_rate * mean
-    step_o[...] = value[0:1, COLS : COLS + 1]
+        here = se_ref[:, s : s + 1] == x
+        total = jnp.where(here, rx[s].astype(jnp.int32), total)
+        step = jnp.where(here, rstep[s], step)
+    share = step * (1.0 / (2 * A * A))
+    total = total.astype(jnp.float32)
+    for t in range(TILES):
+        cols = slice(t * 128, (t + 1) * 128)
+        mean = total[:, cols] * share
+        mean_o[:, cols] = mean
+        new_o[:, cols] = mw_ref[:, cols] - learn_rate * mean
+    step_o[...] = step[0:1, 0:1]
 
 
 def body(expert_grads, round_offsets, slot_expert, master_weight):
@@ -350,12 +355,12 @@
     dma = pltpu.SemaphoreType.DMA
     vmem = pl.BlockSpec(memory_space=pltpu.VMEM)
     hbm = pl.BlockSpec(memory_space=pl.ANY)
-    gathered = pl.pallas_call(
+    gathered, steps = pl.pallas_call(
         kernel,
         name="average",
-        out_shape=pltpu.VMEM((X, ROWS, COLS + 128), f32),
+        out_shape=(pltpu.VMEM((X, ROWS, COLS), jnp.int16), pltpu.VMEM((X, ROWS, 128), f32)),
         in_specs=[hbm, hbm],
-        out_specs=vmem,
+        out_specs=(vmem, vmem),
         scratch_shapes=[
             pltpu.VMEM((2, A, A, ROWS, COLS), bf16),
             pltpu.VMEM((BASE[7], ROWS, COLS), bf16),
@@ -385,8 +390,8 @@
             dma((1,)),
             dma((1,)),
             dma((2,)),
-            dma((1,)),
-            dma((1,)),
+            dma((2,)),
+            dma((2,)),
         ],
         compiler_params=pltpu.CompilerParams(collective_id=0, has_side_effects=True),
     )(expert_grads.reshape(A, A, 2, ROWS, COLS), round_offsets.reshape(A, 128))
@@ -398,10 +403,10 @@
             jax.ShapeDtypeStruct((ROWS, COLS), f32),
             jax.ShapeDtypeStruct((1, 1), f32),
         ),
-        in_specs=[vmem, vmem, vmem],
+        in_specs=[vmem, vmem, vmem, vmem],
         out_specs=(vmem, vmem, vmem),
         compiler_params=pltpu.CompilerParams(vmem_limit_bytes=1024 * 1024),
-    )(gathered, slot_expert.reshape(1, X), master_weight.reshape(ROWS, COLS))
+    )(gathered, steps, slot_expert.reshape(1, X), master_weight.reshape(ROWS, COLS))
     return mean[None], new[None], step
 
 

time: 36.6 us -> 36.4 us (level)
  no operation moved by 1% of the time
where the time goes in v7:
time: 36.4 us; the launch traced here: 36.2 us
  Pallas kernels  35.5 us (98%)
  between operations  0.67 us (2%)
    pallas_call x1, Pallas kernels, body(): pl.pallas_call(kernel, name='average', out_shape=(pltpu.VMEM((X, ROWS, CO...  34.8 us

profile of v7, /device:TPU:8, one launch (start us, length us, event | category | flops | bytes accessed | tf_op | source)
XLA Modules:
  0.0 36.2 jit_solution(15399349993104674270)
XLA Ops:
  0.6 0.0 copy-start
  0.6 0.0 copy-start.1
  0.7 34.8 %average.1 = (s16[4,8,896]{2,1,0:T(8,128)(2,1)S(1)}, f32[4,8,128]{2,1,0:T(8,128)S(1)}) custom-call(bf16[8,8,2,8,896]{4,3,2,1,0:T(8,128)(2,1)} %bitcast.8, s32[8,128]{1,0:T(8,128)} %bitcast.9), custom_call_target="tpu_custom_call" | custom-call | tf_op jit(solution)/shard_map/average/pallas_call | solution.py:358
  35.5 0.0 copy-done
  35.5 0.0 copy-done.1
  35.5 0.7 %finish.1 = (f32[8,896]{1,0:T(8,128)}, f32[8,896]{1,0:T(8,128)}, f32[1,1]{1,0:T(1,128)}) custom-call(s16[4,8,896]{2,1,0:T(8,128)(2,1)S(1)} %get-tuple-element.8.rx, f32[4,8,128]{2,1,0:T(8,128)S(1)} %get-tuple-element.9.rstep, s32[1,4]{1,0:T(1,128)S(1)} %bitcast.7, f32[8,896]{1,0:T(8,128)S(1)} %bitcast.6), custom_call_target="tpu_custom_call" | custom-call | tf_op jit(solution)/shard_map/finish/pallas_call | solution.py:398
Async XLA Ops:
  0.6 34.9 %copy-start = (f32[1,8,896]{2,1,0:T(8,128)S(1)}, f32[1,8,896]{2,1,0:T(8,128)}, u32[]{:S(2)}) copy-start(f32[1,8,896]{2,1,0:T(8,128)} %param.7) | copy-start | bytes 86020
  0.6 34.9 %copy-start.1 = (s32[4]{0:T(128)S(1)}, s32[4]{0:T(128)}, u32[]{:S(2)}) copy-start(s32[4]{0:T(128)} %param.6) | copy-start | bytes 52
